TPU v7x, 256 devices: a whole 4x4x8 slice. The times are simulated.
256 devices in a mesh: gx: 4 (over x_lo, core), gy: 16 (over z, x_hi), gz: 4 (over y).
Axes of the slice: x: 4 (x_hi: 2, x_lo: 2; x = x_hi * 2 + x_lo), y: 4, z: 8, core: 2. Of those that a mesh axis runs over, the one named last changes fastest.
Arguments:
- fields: float32 [5, 64, 128, 512], P(None, 'gz', 'gy', 'gx'), may hold values from -4 to 4
- radius: float32 [8, 64, 128, 512], P(None, 'gz', 'gy', 'gx'), may hold values from 0.4 to 1.5
- weight: float32 [8, 64, 128, 512], P(None, 'gz', 'gy', 'gx'), may hold values from 0.05 to 0.5
- column: int32 [8, 64, 128, 512], P(None, 'gz', 'gy', 'gx'), may hold values from 0 to 127
- counts: int32 [64, 128, 512], P('gz', 'gy', 'gx'), may hold values from 1 to 8
- fall_depth: int32 [8, 64, 128, 4], P(None, 'gz', 'gy', 'gx'), may hold values from 0 to 8, as said below
Outputs:
- new_fields: float32 [5, 64, 128, 512], P(None, 'gz', 'gy', 'gx')
- moments: float32 [3, 64, 128, 512], P(None, 'gz', 'gy', 'gx')
Inputs may be any that keep to these rules, and one draw needn't show every extreme that they name: The droplet in slot s of cell (k, j, i) sits in x cell (i // 128) * 128 + column[s, k, j, i]. Slots s < counts[k, j, i] hold live droplets. The droplets of slot s in cells (k, j, b * 128) to (k, j, (b + 1) * 128 - 1) fall together by fall_depth[s, k, j, b] levels, never below the lowest level: fall_depth[s, k, j, b] <= k; 8 is reached in every draw.
All inputs are finite; a program needn't handle non-finite values. Where the computation divides by a largest or mean magnitude, that divisor is 1e-20 or more.
Results may differ from a plain program's by a relative error of at most 0.00021.
Values sent between devices are 32-bit elements; how exact they have to be, the bound alone decides.
A program may use at most 64 MiB of HBM per device.

v0:
```python
import functools

import jax
import jax.numpy as jnp
from jax import lax
from jax.experimental import pallas as pl
from jax.experimental.pallas import tpu as pltpu
from jax.sharding import PartitionSpec as P

MESH = pl.DeviceIdType.MESH
F32 = jnp.float32
L = 16
DEPTHS = 9
PITCH = 136
WIDE = {0: 0, 1: 1, 3: 2}
NARROW = {2: 0, 4: 1, 5: 2, 6: 3}
SPLITS = (0, 40, 90, 110, 128)


def kernel(
    sizes,
    fields, counts, depth_in, rad_h, wgt_h, col_h,
    out, mom,
    rad, wgt, col, dep, dmat, gmat, ext, fall,
    c0, p0, w0, cq, pq, wq, uq, vq, umq, vmq,
    ta, aa, ba, uinc, vinc, winc, um0, vm0, uminc, vminc,
    tr, pr, lift, pf, uf, vf, wf, pg, ug, vg, wg,
    hx, hy,
    sx, rx, syw, ryw, sya, rya, szw, rzw, sza, rza,
    m1s, m1r, m2s, m2r,
    send_sem, recv_sem, m1_send, m1_recv, m2_send, m2_recv, fall_sem, load_sem,
):
    nx, ny, nz = sizes
    ix, iy, iz = lax.axis_index("gx"), lax.axis_index("gy"), lax.axis_index("gz")

    def near(axis, step):
        i, n = {"gx": (ix, nx), "gy": (iy, ny), "gz": (iz, nz)}[axis]
        return lax.rem(i + (step + n), n)

    lane = lax.broadcasted_iota(jnp.int32, (8, 128), 1)
    row = lax.broadcasted_iota(jnp.int32, (8, 128), 0)
    klo = (iz > 0).astype(F32)
    khi = (iz < nz - 1).astype(F32)

    loads = []
    for a, (src, dst) in enumerate(((rad_h, rad), (wgt_h, wgt), (col_h, col))):
        for s in range(8):
            loads.append(
                pltpu.make_async_copy(
                    src.at[pl.ds(s * 128, 128)], dst.at[pl.ds(s * PITCH, 128)], load_sem.at[a, s]
                )
            )
    for c in loads:
        c.start()

    group1 = [(a, b) for a in range(nx) for b in range(nz) if (a, b) != (0, 0)]
    group2 = list(range(1, ny))
    barrier = pltpu.get_barrier_semaphore()
    for a, b in group1:
        pl.semaphore_signal(
            barrier, inc=1, device_id={"gx": near("gx", a), "gz": near("gz", b)}, device_id_type=MESH
        )
    for a in group2:
        pl.semaphore_signal(barrier, inc=1, device_id={"gy": near("gy", a)}, device_id_type=MESH)

    def roll_l(x, s):
        s = s % 128
        return pltpu.roll(x, s, 1) if s else x

    def roll_s(x, s):
        s = s % 8
        return pltpu.roll(x, s, 0) if s else x

    def xp(q, h, n):
        return roll_l(jnp.where(lane < n, h, q), -n)

    def xm(q, h, n):
        return roll_l(jnp.where(lane >= 128 - n, h, q), n)

    def yp(q, h, n):
        return roll_s(jnp.where(row < n, h, q), -n)

    def ym(q, h, n):
        return roll_s(jnp.where(row >= 8 - n, h, q), n)

    def put_l(message, value, at, width):
        return jnp.where((lane >= at) & (lane < at + width), value, message)

    def put_s(message, value, at, width):
        return jnp.where((row >= at) & (row < at + width), value, message)

    def by_level(fn):
        def group(g, carry):
            state = {}
            for kk in range(8):
                fn(g, kk, g * 8 + kk, state)
            return carry

        lax.fori_loop(0, 2, group, 0)

    def copies(r):
        if r in WIDE:
            w = WIDE[r]
            ysrc, ydst, zsrc, zdst = syw.at[w], ryw.at[w], szw.at[w], rzw.at[w]
            yn = 24 if r == 1 else 16
            zn = 9 if r == 1 else 7
        else:
            w = NARROW[r]
            ysrc, ydst, zsrc, zdst = sya.at[w], rya.at[w], sza.at[w], rza.at[w]
            yn, zn = 4, 2
        made = []
        for d, step in ((0, 1), (1, -1)):
            made.append(
                pltpu.make_async_remote_copy(
                    src_ref=ysrc.at[d, pl.ds(0, yn)], dst_ref=ydst.at[d, pl.ds(0, yn)],
                    send_sem=send_sem.at[r, d], recv_sem=recv_sem.at[r, d],
                    device_id={"gy": near("gy", step)}, device_id_type=MESH,
                )
            )
            made.append(
                pltpu.make_async_remote_copy(
                    src_ref=zsrc.at[d, pl.ds(0, zn)], dst_ref=zdst.at[d, pl.ds(0, zn)],
                    send_sem=send_sem.at[r, 2 + d], recv_sem=recv_sem.at[r, 2 + d],
                    device_id={"gz": near("gz", step)}, device_id_type=MESH,
                )
            )
            made.append(
                pltpu.make_async_remote_copy(
                    src_ref=sx.at[r, d], dst_ref=rx.at[r, d],
                    send_sem=send_sem.at[r, 4 + d], recv_sem=recv_sem.at[r, 4 + d],
                    device_id={"gx": near("gx", step)}, device_id_type=MESH,
                )
            )
        return made

    def send(r):
        made = copies(r)
        for c in made:
            c.start()
        return made

    def arrive(made):
        for c in made:
            c.wait_recv()

    def x_lo(message, kk, a=None, b=None, wind=None, third=None):
        base = 16 * kk
        if a is not None:
            message = put_l(message, roll_l(a, base + 3), base, 3)
        if b is not None:
            message = put_l(message, roll_l(b, base + 6), base + 3, 3)
        if wind is not None:
            message = put_l(message, roll_l(wind, base + 7), base + 6, 1)
        if third is not None:
            message = put_l(message, roll_l(third, base + 11), base + 8, 3)
        return message

    def x_hi(message, kk, a=None, b=None, third=None):
        base = 16 * kk
        if a is not None:
            message = put_l(message, roll_l(a, base), base, 3)
        if b is not None:
            message = put_l(message, roll_l(b, base + 3), base + 3, 3)
        if third is not None:
            message = put_l(message, roll_l(third, base + 8), base + 8, 3)
        return message

    zero = jnp.zeros((8, 128), F32)

    dep[...] = jnp.zeros_like(dep)
    dep[:, :, 0:16] = depth_in[...]

    def prepare(g, kk, k, state):
        c, p, u, v = fields[0, k], fields[1, k], fields[2, k], fields[3, k]
        w = fields[4, k]
        if kk == 7:
            w = w * jnp.where(g == 1, khi, F32(1.0))
        c0[3 + k] = c
        p0[3 + k] = p
        w0[1 + k] = w
        speed = jnp.abs(u) + jnp.abs(v) + jnp.abs(w)
        state["m"] = speed if kk == 0 else jnp.maximum(state["m"], speed)
        state["lo"] = x_lo(state.get("lo", zero), kk, c, p, u)
        state["hi"] = x_hi(state.get("hi", zero), kk, c, p)
        syw[0, 0, k] = put_s(put_s(roll_s(v, -6), roll_s(p, -3), 2, 3), c, 5, 3)
        syw[0, 1, k] = put_s(c, roll_s(p, 3), 3, 3)
        if kk == 7:
            sx[0, 0, g] = state["lo"]
            sx[0, 1, g] = state["hi"]
            pg[g] = state["m"]

    by_level(prepare)
    for n in range(3):
        szw[0, 0, n] = fields[0, 13 + n]
        szw[0, 0, 3 + n] = fields[1, 13 + n]
        szw[0, 1, n] = fields[0, n]
        szw[0, 1, 3 + n] = fields[1, n]
    szw[0, 0, 6] = w0[16]
    szw[0, 1, 6] = zero
    m1s[...] = jnp.max(jnp.maximum(pg[0], pg[1]), axis=0, keepdims=True)

    pl.semaphore_wait(barrier, len(group1) + len(group2))

    first = []
    for o, (a, b) in enumerate(group1):
        first.append(
            pltpu.make_async_remote_copy(
                src_ref=m1s, dst_ref=m1r.at[o], send_sem=m1_send.at[o], recv_sem=m1_recv.at[o],
                device_id={"gx": near("gx", a), "gz": near("gz", b)}, device_id_type=MESH,
            )
        )
    for c in first:
        c.start()
    round0 = send(0)

    for c in loads:
        c.wait()
    target = lax.broadcasted_iota(jnp.int32, (128, 128), 0).astype(F32).astype(jnp.bfloat16)
    row16 = lax.rem(lax.broadcasted_iota(jnp.int32, (16, 128), 0), 8)

    def deposit_row(kj):
        r = rad[pl.ds(kj, 8, stride=PITCH), :]
        w = wgt[pl.ds(kj, 8, stride=PITCH), :]
        c = col[pl.ds(kj, 8, stride=PITCH), :].astype(F32)
        live = row < counts[pl.ds(kj, 1), :]
        number = jnp.where(live, w, 0.0)
        area = number * (r * r)
        mass = area * r
        lhs = []
        for q in (number, area, mass):
            top = q.astype(jnp.bfloat16).astype(F32)
            pair = jnp.concatenate([top, q - top], axis=0)
            lhs.append(
                jnp.concatenate(
                    [jnp.where(row16 == s, pair, 0.0).astype(jnp.bfloat16) for s in range(8)], axis=1
                )
            )
        lhs = jnp.concatenate(lhs, axis=0)
        hot = jnp.concatenate(
            [
                jnp.where(
                    jnp.broadcast_to(c[s : s + 1, :], (128, 128)).astype(jnp.bfloat16) == target,
                    jnp.bfloat16(1.0), jnp.bfloat16(0.0),
                )
                for s in range(8)
            ],
            axis=1,
        )
        got = lax.dot_general(lhs, hot, (((1,), (1,)), ((), ())), preferred_element_type=F32)
        for m in range(3):
            dmat[pl.ds(pl.multiple_of(kj * 24 + 8 * m, 8), 8), :] = got[16 * m : 16 * m + 8] + got[16 * m + 8 : 16 * m + 16]

    def droplets(part):
        def step(i, carry):
            deposit_row(i * 2)
            deposit_row(i * 2 + 1)
            return carry

        lax.fori_loop(SPLITS[part] // 2, SPLITS[part + 1] // 2, step, 0)

    def by_depth():
        def step(k, carry):
            deep = []
            for s in range(8):
                moved = pltpu.roll(dep[s], lax.rem(128 - k, 128), 1)
                deep.append(jnp.broadcast_to(moved[:, 0:1], (8, 128)))
            for m in range(3):
                got = [dmat[pl.ds(k * 192 + 8 * m + s, 8, stride=24), :] for s in range(8)]
                for d in range(DEPTHS):
                    total = jnp.where(deep[0] == d, got[0], 0.0)
                    for s in range(1, 8):
                        total = total + jnp.where(deep[s] == d, got[s], 0.0)
                    gmat[m, d, k] = total
            return carry

        lax.fori_loop(0, L, step, 0)

    droplets(0)

    for c in first:
        c.wait_recv()
    top = m1s[...]
    for o in range(len(group1)):
        top = jnp.maximum(top, m1r[o])
    m2s[...] = top
    second = []
    for o, a in enumerate(group2):
        second.append(
            pltpu.make_async_remote_copy(
                src_ref=m2s, dst_ref=m2r.at[o], send_sem=m2_send.at[o], recv_sem=m2_recv.at[o],
                device_id={"gy": near("gy", a)}, device_id_type=MESH,
            )
        )
    for c in second:
        c.start()

    def flux(a, q):
        central = 37.0 * (q[2] + q[3]) - 8.0 * (q[1] + q[4]) + (q[0] + q[5])
        upwind = 10.0 * (q[3] - q[2]) - 5.0 * (q[4] - q[1]) + (q[5] - q[0])
        return a * central - jnp.abs(a) * upwind

    def advect(q, k, xh, yh, winds):
        own = q[3 + k]
        u, um, v, vm, w, wm = winds
        line = [xm(own, xh[0], 3), xm(own, xh[0], 2), xm(own, xh[0], 1), own,
                xp(own, xh[1], 1), xp(own, xh[1], 2), xp(own, xh[1], 3)]
        total = flux(u, line[1:]) - flux(um, line[:-1])
        line = [ym(own, yh[0], 3), ym(own, yh[0], 2), ym(own, yh[0], 1), own,
                yp(own, yh[1], 1), yp(own, yh[1], 2), yp(own, yh[1], 3)]
        total = total + (flux(v, line[1:]) - flux(vm, line[:-1]))
        line = [q[k + n] for n in range(7)]
        total = total + (flux(w, line[1:]) - flux(wm, line[:-1]))
        return total * F32(-1.0 / 60.0)

    def x_halos(mx, g, kk):
        lo, hi = mx[0, g], mx[1, g]
        base = 16 * kk
        return (roll_l(lo, 125 - base), roll_l(hi, -base)), (roll_l(lo, 122 - base), roll_l(hi, -base - 3)), roll_l(lo, 121 - base)

    def y_halos(my, k):
        lo, hi = my[0, k], my[1, k]
        return (lo, hi), (roll_s(lo, 3), roll_s(hi, -3)), roll_s(lo, 6)

    def lid_at(g, kk):
        return jnp.where(g == 1, khi, F32(1.0)) if kk == 7 else None

    def masked(value, mask):
        return value if mask is None else value * mask

    arrive(round0)
    for n in range(3):
        c0[n] = rzw[0, 0, n] * klo
        p0[n] = rzw[0, 0, 3 + n] * klo
        c0[19 + n] = rzw[0, 1, n] * khi
        p0[19 + n] = rzw[0, 1, 3 + n] * khi
    w0[0] = rzw[0, 0, 6] * klo
    winc[0] = -10.0 * (p0[3] - p0[2]) * klo
    lift[0] = 0.25 * (c0[2] + c0[3]) * klo

    def build(g, kk, k, state):
        lid = lid_at(g, kk)
        xc, xq, xu = x_halos(rx.at[0], g, kk)
        yc, yq, yv = y_halos(ryw.at[0], k)
        p, u, v = p0[3 + k], fields[2, k], fields[3, k]
        w, wm = w0[1 + k], w0[k]
        um, vm = xm(u, xu, 1), ym(v, yv, 1)
        winds = (u, um, v, vm, w, wm)
        t = advect(c0, k, xc, yc, winds)
        q = advect(p0, k, xq, yq, winds)
        du = -10.0 * (xp(p, xq[1], 1) - p)
        dum = -10.0 * (p - xm(p, xq[0], 1))
        dv = -10.0 * (yp(p, yq[1], 1) - p)
        dvm = -10.0 * (p - ym(p, yq[0], 1))
        dw = masked(-10.0 * (p0[4 + k] - p), lid)
        dwm = winc[k]
        up = masked(0.25 * (c0[3 + k] + c0[4 + k]), lid)
        upm = lift[k]
        a = q - 10.0 * ((u - um) + (v - vm) + (w - wm))
        b = -10.0 * ((du - dum) + (dv - dvm) + ((dw + up) - (dwm + upm)))
        ta[k], aa[k], ba[k] = t, a, b
        uinc[k], vinc[k], winc[1 + k], lift[1 + k] = du, dv, dw, up
        um0[k], vm0[k], uminc[k], vminc[k] = um, vm, dum, dvm
        state["lo"] = x_lo(state.get("lo", zero), kk, t, a, None, b)
        state["hi"] = x_hi(state.get("hi", zero), kk, t, a, b)
        syw[1, 0, k] = put_s(put_s(zero, roll_s(a, -3), 2, 3), t, 5, 3)
        syw[1, 1, k] = put_s(put_s(zero, t, 0, 3), roll_s(a, 3), 3, 3)
        at = 4 * (kk % 2)
        if kk % 2 == 0:
            state["ylo"], state["yhi"] = zero, zero
        state["ylo"] = put_s(state["ylo"], roll_s(b, at + 3), at, 3)
        state["yhi"] = put_s(state["yhi"], roll_s(b, at), at, 3)
        if kk % 2 == 1:
            syw[1, 0, 16 + g * 4 + kk // 2] = state["ylo"]
            syw[1, 1, 16 + g * 4 + kk // 2] = state["yhi"]
        if kk == 7:
            sx[1, 0, g] = state["lo"]
            sx[1, 1, g] = state["hi"]

    by_level(build)
    for i, a in enumerate((ta, aa, ba)):
        for n in range(3):
            szw[1, 0, 3 * i + n] = a[13 + n]
            szw[1, 1, 3 * i + n] = a[n]
    round1 = send(1)
    droplets(1)

    for c in second:
        c.wait_recv()
    top = m2s[...]
    for o in range(len(group2)):
        top = jnp.maximum(top, m2r[o])
    top = jnp.broadcast_to(jnp.max(top, axis=1, keepdims=True), (1, 128))
    time_step = jnp.broadcast_to(0.6 / (1.0 + top), (8, 128))

    arrive(round1)
    t1 = time_step * F32(1.0 / 3.0)
    for d in range(2):
        for g in range(2):
            first_part, rate_part = rx[0, d, g], rx[1, d, g]
            slot = lax.rem(lane, 16)
            third = jnp.where((slot >= 3) & (slot < 6), roll_l(rate_part, -5), 0.0)
            hx[d, g] = first_part + t1 * (rate_part + t1 * third)

    def y_section1(g, kk, k, state):
        for d, at in ((0, 2), (1, 3)):
            third = roll_s(ryw[1, d, 16 + g * 4 + kk // 2], at - 4 * (kk % 2))
            third = jnp.where((row >= at) & (row < at + 3), third, 0.0)
            hy[d, k] = ryw[0, d, k] + t1 * (ryw[1, d, k] + t1 * third)
        cq[3 + k] = c0[3 + k] + t1 * ta[k]
        pq[3 + k] = p0[3 + k] + t1 * (aa[k] + t1 * ba[k])
        uq[k] = fields[2, k] + t1 * uinc[k]
        vq[k] = fields[3, k] + t1 * vinc[k]
        umq[k] = um0[k] + t1 * uminc[k]
        vmq[k] = vm0[k] + t1 * vminc[k]
        wq[1 + k] = w0[1 + k] + t1 * (winc[1 + k] + lift[1 + k])

    by_level(y_section1)
    wq[0] = w0[0] + t1 * (winc[0] + lift[0])
    for n in range(3):
        for d, to, keep in ((0, n, klo), (1, 19 + n, khi)):
            cq[to] = c0[to] + (t1 * keep) * rzw[1, d, n]
            pq[to] = p0[to] + (t1 * keep) * (rzw[1, d, 3 + n] + t1 * rzw[1, d, 6 + n])

    def rates(mx, my):
        def step(g, kk, k, state):
            xc, xq, _ = x_halos(mx, g, kk)
            yc, yq, _ = y_halos(my, k)
            winds = (uq[k], umq[k], vq[k], vmq[k], wq[1 + k], wq[k])
            tr[k] = advect(cq, k, xc, yc, winds)
            pr[k] = advect(pq, k, xq, yq, winds)
            lift[1 + k] = masked(0.25 * (cq[3 + k] + cq[4 + k]), lid_at(g, kk))

        by_level(step)
        lift[0] = 0.25 * (cq[2] + cq[3]) * klo

    def narrow_messages(r, g, kk, k, state, p, u, v):
        w = NARROW[r]
        state["lo"] = x_lo(state.get("lo", zero), kk, None, p, u)
        state["hi"] = x_hi(state.get("hi", zero), kk, None, p)
        at = 2 * (kk % 4)
        if kk % 4 == 0:
            state["ylo"], state["yhi"] = zero, zero
        state["ylo"] = put_s(put_s(state["ylo"], roll_s(p, at + 1), at, 1), roll_s(v, at + 2), at + 1, 1)
        state["yhi"] = put_s(state["yhi"], roll_s(p, at), at, 1)
        if kk % 4 == 3:
            sya[w, 0, g * 2 + kk // 4] = state["ylo"]
            sya[w, 1, g * 2 + kk // 4] = state["yhi"]
        if kk == 7:
            sx[r, 0, g] = state["lo"]
            sx[r, 1, g] = state["hi"]

    def narrow_z(r, p, w):
        n = NARROW[r]
        sza[n, 0, 0] = p[16]
        sza[n, 0, 1] = w[16]
        sza[n, 1, 0] = p[1]
        sza[n, 1, 1] = zero

    def first_substep(r, s, to):
        po, uo, vo, wo = to

        def step(g, kk, k, state):
            u = fields[2, k] + s * uinc[k]
            um = um0[k] + s * uminc[k]
            v = fields[3, k] + s * vinc[k]
            vm = vm0[k] + s * vminc[k]
            w = w0[1 + k] + s * (winc[1 + k] + lift[1 + k])
            wm = w0[k] + s * (winc[k] + lift[k])
            p = p0[3 + k] + s * (pr[k] - 10.0 * ((u - um) + (v - vm) + (w - wm)))
            po[1 + k], uo[k], vo[k], wo[1 + k] = p, u, v, w
            narrow_messages(r, g, kk, k, state, p, u, v)

        by_level(step)
        narrow_z(r, po, wo)
        return send(r)

    def next_substep(r, made, s, source, finish):
        n = NARROW[r]
        ps, us, vs, ws = source
        arrive(made)
        ps[0] = rza[n, 0, 0] * klo
        ws[0] = rza[n, 0, 1] * klo
        ps[17] = rza[n, 1, 0] * khi
        s10 = s * 10.0

        def step(g, kk, k, state):
            lid = lid_at(g, kk)
            _, xq, xu = x_halos(rx.at[r], g, kk)
            ylo, yhi = rya[n, 0, g * 2 + kk // 4], rya[n, 1, g * 2 + kk // 4]
            at = 2 * (kk % 4)
            p, u, v = ps[1 + k], us[k], vs[k]
            un = u - s10 * (xp(p, xq[1], 1) - p)
            um = xm(u, xu, 1) - s10 * (p - xm(p, xq[0], 1))
            vn = v - s10 * (yp(p, roll_s(yhi, -at), 1) - p)
            vm = ym(v, roll_s(ylo, 6 - at), 1) - s10 * (p - ym(p, roll_s(ylo, 7 - at), 1))
            wn = ws[1 + k] + s * lift[1 + k] - masked(s10 * (ps[2 + k] - p), lid)
            below = s10 * (p - ps[k])
            if kk == 0:
                below = below * jnp.where(g == 0, klo, F32(1.0))
            wm = ws[k] + s * lift[k] - below
            pn = p + s * (pr[k] - 10.0 * ((un - um) + (vn - vm) + (wn - wm)))
            finish(g, kk, k, state, pn, un, vn, wn)

        by_level(step)

    rates(hx, hy)
    t2 = time_step * F32(0.25)
    round2 = first_substep(2, t2, (pf, uf, vf, wf))
    droplets(2)

    half = time_step * F32(0.5)

    def finish2(g, kk, k, state, p, u, v, w):
        c = c0[3 + k] + half * tr[k]
        cq[3 + k], pq[3 + k], uq[k], vq[k], wq[1 + k] = c, p, u, v, w
        state["lo"] = x_lo(state.get("lo", zero), kk, c, p, u)
        state["hi"] = x_hi(state.get("hi", zero), kk, c, p)
        syw[2, 0, k] = put_s(put_s(roll_s(v, -6), roll_s(p, -3), 2, 3), c, 5, 3)
        syw[2, 1, k] = put_s(c, roll_s(p, 3), 3, 3)
        if kk == 7:
            sx[3, 0, g] = state["lo"]
            sx[3, 1, g] = state["hi"]

    next_substep(2, round2, t2, (pf, uf, vf, wf), finish2)
    for n in range(3):
        szw[2, 0, n] = cq[16 + n]
        szw[2, 0, 3 + n] = pq[16 + n]
        szw[2, 1, n] = cq[3 + n]
        szw[2, 1, 3 + n] = pq[3 + n]
    szw[2, 0, 6] = wq[16]
    szw[2, 1, 6] = zero
    round3 = send(3)
    droplets(3)
    by_depth()

    arrive(round3)
    for n in range(3):
        cq[n] = rzw[2, 0, n] * klo
        pq[n] = rzw[2, 0, 3 + n] * klo
        cq[19 + n] = rzw[2, 1, n] * khi
        pq[19 + n] = rzw[2, 1, 3 + n] * khi
    wq[0] = rzw[2, 0, 6] * klo

    def face_winds(g, kk, k, state):
        _, _, xu = x_halos(rx.at[3], g, kk)
        _, _, yv = y_halos(ryw.at[2], k)
        umq[k] = xm(uq[k], xu, 1)
        vmq[k] = ym(vq[k], yv, 1)

    by_level(face_winds)
    rates(rx.at[3], ryw.at[2])
    t3 = time_step * F32(0.25)
    round4 = first_substep(4, t3, (pf, uf, vf, wf))

    for k in range(L):
        c = c0[3 + k] + time_step * tr[k]
        out[0, k] = c
        growth = jnp.minimum(jnp.exp(0.3 * c), F32(3.0e38))
        ta[k] = growth
        aa[k] = jnp.sqrt(growth)

    def landed(t):
        totals = [None, None, None]
        for k in range(max(t, 0), min(t + DEPTHS, L)):
            d = k - t
            grow, root = ta[k], aa[k]
            parts = (gmat[0, d, k], gmat[1, d, k] * grow, gmat[2, d, k] * grow * root)
            totals = [a if b is None else b + a for a, b in zip(parts, totals)]
        return totals

    for t in range(-8, 0):
        for m, value in enumerate(landed(t)):
            ext[m, t + 8] = value
    dropped = pltpu.make_async_remote_copy(
        src_ref=ext, dst_ref=fall, send_sem=fall_sem.at[0], recv_sem=fall_sem.at[1],
        device_id={"gz": near("gz", -1)}, device_id_type=MESH,
    )
    dropped.start()
    for t in range(0, L):
        for m, value in enumerate(landed(t)):
            mom[m, t] = value

    def passing(r, to):
        po, uo, vo, wo = to

        def finish(g, kk, k, state, p, u, v, w):
            po[1 + k], uo[k], vo[k], wo[1 + k] = p, u, v, w
            narrow_messages(r, g, kk, k, state, p, u, v)

        return finish

    next_substep(4, round4, t3, (pf, uf, vf, wf), passing(5, (pg, ug, vg, wg)))
    narrow_z(5, pg, wg)
    round5 = send(5)
    next_substep(5, round5, t3, (pg, ug, vg, wg), passing(6, (pf, uf, vf, wf)))
    narrow_z(6, pf, wf)
    round6 = send(6)
    dropped.wait_recv()
    for m in range(3):
        for n in range(8):
            mom[m, 8 + n] = mom[m, 8 + n] + fall[m, n] * khi

    def last(g, kk, k, state, p, u, v, w):
        out[1, k], out[2, k], out[3, k], out[4, k] = p, u, v, w

    next_substep(6, round6, t3, (pf, uf, vf, wf), last)

    dropped.wait_send()
    for made in (first, second, round0, round1, round2, round3, round4, round5, round6):
        for c in made:
            c.wait_send()


def solution(mesh):
    sizes = (mesh.shape["gx"], mesh.shape["gy"], mesh.shape["gz"])
    nx, ny, nz = sizes
    vm = lambda *shape: pltpu.VMEM(shape + (8, 128), F32)
    dma = pltpu.SemaphoreType.DMA
    scratch = [
        pltpu.VMEM((8 * PITCH, 128), F32), pltpu.VMEM((8 * PITCH, 128), F32), pltpu.VMEM((8 * PITCH, 128), jnp.int32),
        pltpu.VMEM((8, 8, 128), jnp.int32), pltpu.VMEM((128 * 24, 128), F32), vm(3, DEPTHS, L), vm(3, 8), vm(3, 8),
        vm(22), vm(22), vm(17), vm(22), vm(22), vm(17), vm(16), vm(16), vm(16), vm(16),
        vm(16), vm(16), vm(16), vm(16), vm(16), vm(17), vm(16), vm(16), vm(16), vm(16),
        vm(16), vm(16), vm(17), vm(18), vm(16), vm(16), vm(17), vm(18), vm(16), vm(16), vm(17),
        vm(2, 2), vm(2, 16),
        vm(7, 2, 2), vm(7, 2, 2), vm(3, 2, 24), vm(3, 2, 24), vm(4, 2, 4), vm(4, 2, 4),
        vm(3, 2, 9), vm(3, 2, 9), vm(4, 2, 2), vm(4, 2, 2),
        pltpu.VMEM((1, 128), F32), pltpu.VMEM((nx * nz - 1, 1, 128), F32),
        pltpu.VMEM((1, 128), F32), pltpu.VMEM((ny - 1, 1, 128), F32),
        dma((7, 6)), dma((7, 6)), dma((nx * nz - 1,)), dma((nx * nz - 1,)), dma((ny - 1,)), dma((ny - 1,)),
        dma((2,)), dma((3, 8)),
    ]
    vmem = pl.BlockSpec(memory_space=pltpu.VMEM)
    hbm = pl.BlockSpec(memory_space=pl.ANY)

    def per_device(fields, radius, weight, column, counts, fall_depth):
        return pl.pallas_call(
            functools.partial(kernel, sizes),
            out_shape=(
                jax.ShapeDtypeStruct((5, L, 8, 128), F32),
                jax.ShapeDtypeStruct((3, L, 8, 128), F32),
            ),
            in_specs=[vmem, vmem, vmem, hbm, hbm, hbm],
            out_specs=(vmem, vmem),
            scratch_shapes=scratch,
            compiler_params=pltpu.CompilerParams(collective_id=0, has_side_effects=True),
            name="slab_step",
        )(
            fields,
            counts.reshape(128, 128),
            jnp.transpose(fall_depth[:, :, :, 0], (0, 2, 1)),
            radius.reshape(1024, 128),
            weight.reshape(1024, 128),
            column.reshape(1024, 128),
        )

    cut = P(None, "gz", "gy", "gx")
    return jax.shard_map(
        per_device,
        mesh=mesh,
        in_specs=(cut, cut, cut, cut, P("gz", "gy", "gx"), cut),
        out_specs=(cut, cut),
        check_vma=False,
    )
```

profile of v0, /device:TPU:1, one launch (start us, length us, event | category | flops | bytes accessed | tf_op | source)
XLA Modules:
  0.0 58.5 jit_solution(1120046158405930342)
XLA Ops:
  0.6 55.4 %slab_step.1 = (f32[5,16,8,128]{3,2,1,0:T(8,128)}, f32[3,16,8,128]{3,2,1,0:T(8,128)}) custom-call(f32[5,16,8,128]{3,2,1,0:T(8,128)} %fields.1, s32[128,128]{1,0:T(8,128)} %bitcast.10, s32[8,8,16]{2,1,0:T(8,128)} %bitcast.11, f32[1024,128]{1,0:T(8,128)} %bitcast.7, f32[1024,128]{1,0:T(8,128)} %bitcast.8, s32[1024,128]{1,0:T(8,128)} %bitcast.9), custom_call_target="tpu_custom_call" | custom-call | tf_op jit(solution)/shard_map/slab_step/pallas_call | solution.py:637
  56.0 0.0 copy-start
  56.0 1.8 %copy.10 = f32[5,16,8,128]{3,2,1,0:T(8,128)} copy(f32[5,16,8,128]{3,2,1,0:T(8,128)} %get-tuple-element.4) | data formatting | bytes 655360
  57.8 0.0 copy-done
  57.8 0.7 %copy.11 = f32[3,16,8,128]{3,2,1,0:T(8,128)} copy(f32[3,16,8,128]{3,2,1,0:T(8,128)S(1)} %copy-done) | data formatting | bytes 393216
Async XLA Ops:
  56.0 1.8 %copy-start = (f32[3,16,8,128]{3,2,1,0:T(8,128)S(1)}, f32[3,16,8,128]{3,2,1,0:T(8,128)}, u32[]{:S(2)}) copy-start(f32[3,16,8,128]{3,2,1,0:T(8,128)} %get-tuple-element.5) | copy-start | bytes 589828
where the time goes:
time: 59.5 us; the launch traced here: 58.5 us
  Pallas kernels  55.4 us (93%)
  local copies, waits for them, and re-layouts  2.44 us (4%)
  between operations  0.65 us (1%)
    pallas_call x1, Pallas kernels, per_device(): pl.pallas_call(functools.partial(kernel, sizes), out_shape=(jax.ShapeDtyp...  55.4 us
    unnamed x4, local copies, waits for them, and re-layouts  2.44 us

commit v1 on v0

v1 whole, which is shorter than its diff:
```python
import functools

import jax
import jax.numpy as jnp
from jax import lax
from jax.experimental import pallas as pl
from jax.experimental.pallas import tpu as pltpu
from jax.sharding import PartitionSpec as P

MESH = pl.DeviceIdType.MESH
F32 = jnp.float32
L = 16
DEPTHS = 9
PITCH = 136
Y_TILES = {0: (14, 12), 1: (18, 18), 7: (6, 6), 3: (6, 6), 2: (2, 2), 4: (2, 2), 5: (2, 2), 6: (2, 2)}
Z_TILES = {0: (7, 6), 1: (9, 9), 7: (3, 3), 3: (3, 3), 2: (1, 1), 4: (1, 1), 5: (1, 1), 6: (1, 1)}
Y_AT = {0: 0, 1: 14, 7: 32, 3: 38, 2: 44, 4: 46, 5: 48, 6: 50}
Z_AT = {0: 0, 1: 7, 7: 16, 3: 19, 2: 22, 4: 23, 5: 24, 6: 25}
Y_ALL, Z_ALL = 52, 26
SPLITS = (0, 24, 58, 80, 100, 128)


def kernel(
    sizes,
    fields_h, counts_h, depth_h, rad_h, wgt_h, col_h,
    out, mom,
    fields, counts, depth_in, rad, wgt, col, dep, dmat, gmat, ext, fall,
    c0, p0, w0, cq, pq, peak,
    ta, aa, ba, uinc, vinc, winc, um0, vm0, uminc, vminc,
    tr, lift, pf, pg, uf, vf, umf, vmf, wf, ug, vg, umg, vmg, wg,
    hx, hy,
    sx, rx, sy, ry, sz, rz,
    m1s, m1r, m2s, m2r,
    send_sem, recv_sem, m1_send, m1_recv, m2_send, m2_recv, fall_sem, load_sem, field_sem,
):
    nx, ny, nz = sizes
    ix, iy, iz = lax.axis_index("gx"), lax.axis_index("gy"), lax.axis_index("gz")

    def near(axis, step):
        i, n = {"gx": (ix, nx), "gy": (iy, ny), "gz": (iz, nz)}[axis]
        return lax.rem(i + (step + n), n)

    group1 = [(a, b) for a in range(nx) for b in range(nz) if (a, b) != (0, 0)]
    group2 = list(range(1, ny))
    barrier = pltpu.get_barrier_semaphore()
    for a in group2:
        pl.semaphore_signal(barrier, inc=1, device_id={"gy": near("gy", a)}, device_id_type=MESH)
    for a, b in group1:
        pl.semaphore_signal(
            barrier, inc=1, device_id={"gx": near("gx", a), "gz": near("gz", b)}, device_id_type=MESH
        )

    early = [
        pltpu.make_async_copy(src, dst, field_sem.at[n])
        for n, (src, dst) in enumerate(((fields_h, fields), (counts_h, counts), (depth_h, depth_in)))
    ]
    loads = []
    for a, (src, dst) in enumerate(((rad_h, rad), (wgt_h, wgt), (col_h, col))):
        for s in range(8):
            loads.append(
                pltpu.make_async_copy(
                    src.at[pl.ds(s * 128, 128)], dst.at[pl.ds(s * PITCH, 128)], load_sem.at[a, s]
                )
            )
    for c in early:
        c.start()

    lane = lax.broadcasted_iota(jnp.int32, (8, 128), 1)
    row = lax.broadcasted_iota(jnp.int32, (8, 128), 0)
    klo = (iz > 0).astype(F32)
    khi = (iz < nz - 1).astype(F32)
    zero = jnp.zeros((8, 128), F32)

    def roll_l(x, s):
        s = s % 128
        return pltpu.roll(x, s, 1) if s else x

    def roll_s(x, s):
        s = s % 8
        return pltpu.roll(x, s, 0) if s else x

    def xp(q, h, n):
        return roll_l(jnp.where(lane < n, h, q), -n)

    def xm(q, h, n):
        return roll_l(jnp.where(lane >= 128 - n, h, q), n)

    def yp(q, h, n):
        return roll_s(jnp.where(row < n, h, q), -n)

    def ym(q, h, n):
        return roll_s(jnp.where(row >= 8 - n, h, q), n)

    def put_l(message, value, at, width):
        return jnp.where((lane >= at) & (lane < at + width), value, message)

    def by_level(fn):
        def group(g, carry):
            state = {}
            for kk in range(8):
                fn(g, kk, g * 8 + kk, state)
            return carry

        lax.fori_loop(0, 2, group, 0)

    def copies(r):
        made = []
        for d, step in ((0, 1), (1, -1)):
            y, z = pl.ds(Y_AT[r], Y_TILES[r][d]), pl.ds(Z_AT[r], Z_TILES[r][d])
            for i, (src, dst, axis) in enumerate(
                ((sy.at[d, y], ry.at[d, y], "gy"), (sz.at[d, z], rz.at[d, z], "gz"), (sx.at[r, d], rx.at[r, d], "gx"))
            ):
                made.append(
                    pltpu.make_async_remote_copy(
                        src_ref=src, dst_ref=dst,
                        send_sem=send_sem.at[r, 2 * i + d], recv_sem=recv_sem.at[r, 2 * i + d],
                        device_id={axis: near(axis, step)}, device_id_type=MESH,
                    )
                )
        return made

    def send(r):
        made = copies(r)
        for c in made:
            c.start()
        return made

    def arrive(made):
        for c in made:
            c.wait_recv()

    def x_pack(state, r, g, kk, a=None, b=None, wind=None, third=None):
        base = 16 * kk
        lo, hi = state.get("xlo", zero), state.get("xhi", zero)
        for value, at in ((a, 0), (b, 3), (third, 8)):
            if value is not None:
                lo = put_l(lo, roll_l(value, base + at + 3), base + at, 3)
                hi = put_l(hi, roll_l(value, base + at), base + at, 3)
        if wind is not None:
            lo = put_l(lo, roll_l(wind, base + 7), base + 6, 1)
        state["xlo"], state["xhi"] = lo, hi
        if kk == 7:
            sx[r, 0, g] = lo
            sx[r, 1, g] = hi

    def y_pack3(state, name, start, g, kk, q):
        t, o = divmod(3 * kk, 8)
        for d, moved in ((0, roll_s(q, o - 5)), (1, roll_s(q, o))):
            key = (name, d)
            tiles = state.setdefault(key, [None, None, None])
            if tiles[t] is None:
                tiles[t] = moved
            else:
                tiles[t] = jnp.where(row >= o, moved, tiles[t])
            if o > 5:
                tiles[t + 1] = moved
            if o >= 5:
                sy[d, start + g * 3 + t] = tiles[t]

    def y_halo3(ref, start, g, kk):
        t, o = divmod(3 * kk, 8)
        got = []
        for d in range(2):
            value = ref[d, start + g * 3 + t]
            if o > 5:
                value = jnp.where(row >= o, value, ref[d, start + g * 3 + t + 1])
            got.append(roll_s(value, 5 - o if d == 0 else -o))
        return got

    def y_pack1(state, name, start, g, kk, last=None, first=None):
        for d, value, by in ((0, last, kk - 7), (1, first, kk)):
            if value is not None:
                key = (name, d)
                moved = roll_s(value, by)
                state[key] = moved if kk == 0 else jnp.where(row >= kk, moved, state[key])
                if kk == 7:
                    sy[d, start + g] = state[key]

    def x_halos(mx, g, kk):
        lo, hi = mx[0, g], mx[1, g]
        base = 16 * kk
        return (roll_l(lo, 125 - base), roll_l(hi, -base)), (roll_l(lo, 122 - base), roll_l(hi, -base - 3)), roll_l(lo, 121 - base)

    def x_halo(ref, at, g, kk):
        base = 16 * kk + at
        return roll_l(ref[0, g], 125 - base), roll_l(ref[1, g], -base)

    def lid_at(g, kk):
        return jnp.where(g == 1, khi, F32(1.0)) if kk == 7 else None

    def masked(value, mask):
        return value if mask is None else value * mask

    early[0].wait()
    for c in loads:
        c.start()

    def prepare(g, kk, k, state):
        c, p, u, v = fields[0, k], fields[1, k], fields[2, k], fields[3, k]
        w = masked(fields[4, k], lid_at(g, kk))
        c0[3 + k] = c
        p0[3 + k] = p
        w0[1 + k] = w
        speed = jnp.abs(u) + jnp.abs(v) + jnp.abs(w)
        state["m"] = speed if kk == 0 else jnp.maximum(state["m"], speed)
        x_pack(state, 0, g, kk, c, p, u)
        y_pack3(state, "c", Y_AT[0], g, kk, c)
        y_pack3(state, "p", Y_AT[0] + 6, g, kk, p)
        y_pack1(state, "v", Y_AT[0] + 12, g, kk, last=v)
        if kk == 7:
            peak[g] = state["m"]

    by_level(prepare)
    for n in range(3):
        sz[0, Z_AT[0] + n] = fields[0, 13 + n]
        sz[0, Z_AT[0] + 3 + n] = fields[1, 13 + n]
        sz[1, Z_AT[0] + n] = fields[0, n]
        sz[1, Z_AT[0] + 3 + n] = fields[1, n]
    sz[0, Z_AT[0] + 6] = w0[16]
    m1s[...] = jnp.max(jnp.maximum(peak[0], peak[1]), axis=0, keepdims=True)

    target = lax.broadcasted_iota(jnp.int32, (128, 128), 0).astype(F32).astype(jnp.bfloat16)
    row16 = lax.rem(lax.broadcasted_iota(jnp.int32, (16, 128), 0), 8)

    def deposit_row(kj):
        r = rad[pl.ds(kj, 8, stride=PITCH), :]
        w = wgt[pl.ds(kj, 8, stride=PITCH), :]
        c = col[pl.ds(kj, 8, stride=PITCH), :].astype(F32)
        live = row < counts[pl.ds(kj, 1), :]
        number = jnp.where(live, w, 0.0)
        area = number * (r * r)
        mass = area * r
        lhs = []
        for q in (number, area, mass):
            top = q.astype(jnp.bfloat16).astype(F32)
            pair = jnp.concatenate([top, q - top], axis=0)
            lhs.append(
                jnp.concatenate(
                    [jnp.where(row16 == s, pair, 0.0).astype(jnp.bfloat16) for s in range(8)], axis=1
                )
            )
        lhs = jnp.concatenate(lhs, axis=0)
        hot = jnp.concatenate(
            [
                jnp.where(
                    jnp.broadcast_to(c[s : s + 1, :], (128, 128)).astype(jnp.bfloat16) == target,
                    jnp.bfloat16(1.0), jnp.bfloat16(0.0),
                )
                for s in range(8)
            ],
            axis=1,
        )
        got = lax.dot_general(lhs, hot, (((1,), (1,)), ((), ())), preferred_element_type=F32)
        for m in range(3):
            dmat[pl.ds(pl.multiple_of(kj * 24 + 8 * m, 8), 8), :] = got[16 * m : 16 * m + 8] + got[16 * m + 8 : 16 * m + 16]

    def droplets(part):
        def step(i, carry):
            deposit_row(i * 2)
            deposit_row(i * 2 + 1)
            return carry

        lax.fori_loop(SPLITS[part] // 2, SPLITS[part + 1] // 2, step, 0)

    def by_depth():
        def step(k, carry):
            deep = []
            for s in range(8):
                moved = pltpu.roll(dep[s], lax.rem(128 - k, 128), 1)
                deep.append(jnp.broadcast_to(moved[:, 0:1], (8, 128)))
            for m in range(3):
                got = [dmat[pl.ds(k * 192 + 8 * m + s, 8, stride=24), :] for s in range(8)]
                for d in range(DEPTHS):
                    total = jnp.where(deep[0] == d, got[0], 0.0)
                    for s in range(1, 8):
                        total = total + jnp.where(deep[s] == d, got[s], 0.0)
                    gmat[m, d, k] = total
            return carry

        lax.fori_loop(0, L, step, 0)

    pl.semaphore_wait(barrier, len(group1) + len(group2))

    first = []
    for o, (a, b) in enumerate(group1):
        first.append(
            pltpu.make_async_remote_copy(
                src_ref=m1s, dst_ref=m1r.at[o], send_sem=m1_send.at[o], recv_sem=m1_recv.at[o],
                device_id={"gx": near("gx", a), "gz": near("gz", b)}, device_id_type=MESH,
            )
        )
    for c in first:
        c.start()
    round0 = send(0)
    for c in early[1:] + loads:
        c.wait()
    dep[...] = jnp.zeros_like(dep)
    dep[:, :, 0:16] = depth_in[...]
    droplets(0)

    def flux(a, q):
        central = 37.0 * (q[2] + q[3]) - 8.0 * (q[1] + q[4]) + (q[0] + q[5])
        upwind = 10.0 * (q[3] - q[2]) - 5.0 * (q[4] - q[1]) + (q[5] - q[0])
        return a * central - jnp.abs(a) * upwind

    def advect(q, k, xh, yh, winds):
        own = q[3 + k]
        u, um, v, vm, w, wm = winds
        line = [xm(own, xh[0], 3), xm(own, xh[0], 2), xm(own, xh[0], 1), own,
                xp(own, xh[1], 1), xp(own, xh[1], 2), xp(own, xh[1], 3)]
        total = flux(u, line[1:]) - flux(um, line[:-1])
        line = [ym(own, yh[0], 3), ym(own, yh[0], 2), ym(own, yh[0], 1), own,
                yp(own, yh[1], 1), yp(own, yh[1], 2), yp(own, yh[1], 3)]
        total = total + (flux(v, line[1:]) - flux(vm, line[:-1]))
        line = [q[k + n] for n in range(7)]
        total = total + (flux(w, line[1:]) - flux(wm, line[:-1]))
        return total * F32(-1.0 / 60.0)

    arrive(round0)
    for n in range(3):
        for d, to, keep in ((0, n, klo), (1, 19 + n, khi)):
            c0[to] = rz[d, Z_AT[0] + n] * keep
            p0[to] = rz[d, Z_AT[0] + 3 + n] * keep
    w0[0] = rz[0, Z_AT[0] + 6] * klo
    winc[0] = -10.0 * (p0[3] - p0[2]) * klo
    lift[0] = 0.25 * (c0[2] + c0[3]) * klo

    def build(g, kk, k, state):
        lid = lid_at(g, kk)
        xc, xq, xu = x_halos(rx.at[0], g, kk)
        yc = y_halo3(ry, Y_AT[0], g, kk)
        yq = y_halo3(ry, Y_AT[0] + 6, g, kk)
        yv = roll_s(ry[0, Y_AT[0] + 12 + g], 7 - kk)
        p, u, v = p0[3 + k], fields[2, k], fields[3, k]
        w, wm = w0[1 + k], w0[k]
        um, vm = xm(u, xu, 1), ym(v, yv, 1)
        winds = (u, um, v, vm, w, wm)
        t = advect(c0, k, xc, yc, winds)
        q = advect(p0, k, xq, yq, winds)
        du = -10.0 * (xp(p, xq[1], 1) - p)
        dum = -10.0 * (p - xm(p, xq[0], 1))
        dv = -10.0 * (yp(p, yq[1], 1) - p)
        dvm = -10.0 * (p - ym(p, yq[0], 1))
        dw = masked(-10.0 * (p0[4 + k] - p), lid)
        dwm = winc[k]
        up = masked(0.25 * (c0[3 + k] + c0[4 + k]), lid)
        upm = lift[k]
        a = q - 10.0 * ((u - um) + (v - vm) + (w - wm))
        b = -10.0 * ((du - dum) + (dv - dvm) + ((dw + up) - (dwm + upm)))
        ta[k], aa[k], ba[k] = t, a, b
        uinc[k], vinc[k], winc[1 + k], lift[1 + k] = du, dv, dw, up
        um0[k], vm0[k], uminc[k], vminc[k] = um, vm, dum, dvm
        x_pack(state, 1, g, kk, t, a, None, b)
        for i, value in enumerate((t, a, b)):
            y_pack3(state, i, Y_AT[1] + 6 * i, g, kk, value)

    by_level(build)
    for i, a in enumerate((ta, aa, ba)):
        for n in range(3):
            sz[0, Z_AT[1] + 3 * i + n] = a[13 + n]
            sz[1, Z_AT[1] + 3 * i + n] = a[n]
    round1 = send(1)

    for c in first:
        c.wait_recv()
    top = m1s[...]
    for o in range(len(group1)):
        top = jnp.maximum(top, m1r[o])
    m2s[...] = top
    second = []
    for o, a in enumerate(group2):
        second.append(
            pltpu.make_async_remote_copy(
                src_ref=m2s, dst_ref=m2r.at[o], send_sem=m2_send.at[o], recv_sem=m2_recv.at[o],
                device_id={"gy": near("gy", a)}, device_id_type=MESH,
            )
        )
    for c in second:
        c.start()

    droplets(1)

    for c in second:
        c.wait_recv()
    top = m2s[...]
    for o in range(len(group2)):
        top = jnp.maximum(top, m2r[o])
    top = jnp.broadcast_to(jnp.max(top, axis=1, keepdims=True), (1, 128))
    time_step = jnp.broadcast_to(0.6 / (1.0 + top), (8, 128))

    arrive(round1)
    t1 = time_step * F32(1.0 / 3.0)
    slot = lax.rem(lane, 16)
    for d in range(2):
        for g in range(2):
            third = jnp.where((slot >= 3) & (slot < 6), roll_l(rx[1, d, g], -5), 0.0)
            hx[d, g] = rx[0, d, g] + t1 * (rx[1, d, g] + t1 * third)
        for n in range(6):
            hy[d, n] = ry[d, n] + t1 * ry[d, 14 + n]
            hy[d, 6 + n] = ry[d, 6 + n] + t1 * (ry[d, 20 + n] + t1 * ry[d, 26 + n])

    def section1(g, kk, k, state):
        cq[3 + k] = c0[3 + k] + t1 * ta[k]
        pq[3 + k] = p0[3 + k] + t1 * (aa[k] + t1 * ba[k])
        uf[k] = fields[2, k] + t1 * uinc[k]
        vf[k] = fields[3, k] + t1 * vinc[k]
        umf[k] = um0[k] + t1 * uminc[k]
        vmf[k] = vm0[k] + t1 * vminc[k]
        wf[1 + k] = w0[1 + k] + t1 * (winc[1 + k] + lift[1 + k])

    by_level(section1)
    wf[0] = w0[0] + t1 * (winc[0] + lift[0])
    for n in range(3):
        for d, to, keep in ((0, n, klo), (1, 19 + n, khi)):
            cq[to] = c0[to] + (t1 * keep) * rz[d, Z_AT[1] + n]
            pq[to] = p0[to] + (t1 * keep) * (rz[d, Z_AT[1] + 3 + n] + t1 * rz[d, Z_AT[1] + 6 + n])

    def tracer_rates(mx, my, start, old, finish):
        u, v, um, vm, w = old

        def step(g, kk, k, state):
            winds = (u[k], um[k], v[k], vm[k], w[1 + k], w[k])
            finish(g, kk, k, state, advect(cq, k, x_halo(mx, 0, g, kk), y_halo3(my, start, g, kk), winds))

        by_level(step)

    def lifts():
        lift[0] = 0.25 * (cq[2] + cq[3]) * klo

        def step(g, kk, k, state):
            lift[1 + k] = masked(0.25 * (cq[3 + k] + cq[4 + k]), lid_at(g, kk))

        by_level(step)

    def narrow(r, g, kk, k, state, p):
        x_pack(state, r, g, kk, None, p)
        y_pack1(state, "p", Y_AT[r], g, kk, last=p, first=p)

    def narrow_send(r, p):
        sz[0, Z_AT[r]] = p[16]
        sz[1, Z_AT[r]] = p[1]
        return send(r)

    def first_substep(r, s, mx, my, start, old, new, rate_ref):
        u_, v_, um_, vm_, w_ = old
        un_, vn_, umn_, vmn_, wn_ = new
        wn_[0] = w0[0] + s * (winc[0] + lift[0])

        def step(g, kk, k, state):
            winds = (u_[k], um_[k], v_[k], vm_[k], w_[1 + k], w_[k])
            rate = advect(pq, k, x_halo(mx, 3, g, kk), y_halo3(my, start, g, kk), winds)
            rate_ref[k] = rate
            u = fields[2, k] + s * uinc[k]
            um = um0[k] + s * uminc[k]
            v = fields[3, k] + s * vinc[k]
            vm = vm0[k] + s * vminc[k]
            w = w0[1 + k] + s * (winc[1 + k] + lift[1 + k])
            wm = w0[k] + s * (winc[k] + lift[k])
            p = p0[3 + k] + s * (rate - 10.0 * ((u - um) + (v - vm) + (w - wm)))
            pf[1 + k], un_[k], vn_[k], umn_[k], vmn_[k], wn_[1 + k] = p, u, v, um, vm, w
            narrow(r, g, kk, k, state, p)

        by_level(step)
        return narrow_send(r, pf)

    def next_substep(r, made, s, ps, winds, rate_ref, finish):
        u_, v_, um_, vm_, w_ = winds
        s10 = s * 10.0
        arrive(made)
        ps[0] = rz[0, Z_AT[r]] * klo
        ps[17] = rz[1, Z_AT[r]] * khi
        w_[0] = w_[0] + s * lift[0] - (s10 * klo) * (ps[1] - ps[0])

        def step(g, kk, k, state):
            lid = lid_at(g, kk)
            xq = x_halo(rx.at[r], 3, g, kk)
            p = ps[1 + k]
            ylo, yhi = roll_s(ry[0, Y_AT[r] + g], 7 - kk), roll_s(ry[1, Y_AT[r] + g], -kk)
            u = u_[k] - s10 * (xp(p, xq[1], 1) - p)
            um = um_[k] - s10 * (p - xm(p, xq[0], 1))
            v = v_[k] - s10 * (yp(p, yhi, 1) - p)
            vm = vm_[k] - s10 * (p - ym(p, ylo, 1))
            w = w_[1 + k] + s * lift[1 + k] - masked(s10 * (ps[2 + k] - p), lid)
            wm = state["w"] if kk else w_[k]
            state["w"] = w
            pn = p + s * (rate_ref[k] - 10.0 * ((u - um) + (v - vm) + (w - wm)))
            finish(g, kk, k, state, pn, u, v, um, vm, w)

        by_level(step)

    state_f = (uf, vf, umf, vmf, wf)
    state_g = (ug, vg, umg, vmg, wg)

    t2 = time_step * F32(0.25)
    half = time_step * F32(0.5)
    lifts()
    round2 = first_substep(2, t2, hx, hy, 6, state_f, state_g, aa)

    def tracer2(g, kk, k, state, rate):
        c = c0[3 + k] + half * rate
        tr[k] = c
        x_pack(state, 7, g, kk, c)
        y_pack3(state, "c", Y_AT[7], g, kk, c)

    tracer_rates(hx, hy, 0, state_f, tracer2)
    for n in range(3):
        sz[0, Z_AT[7] + n] = tr[13 + n]
        sz[1, Z_AT[7] + n] = tr[n]
    round7 = send(7)
    droplets(2)

    def finish2(g, kk, k, state, p, u, v, um, vm, w):
        pq[3 + k] = p
        ug[k], vg[k], umg[k], vmg[k], wg[1 + k] = u, v, um, vm, w
        cq[3 + k] = tr[k]
        x_pack(state, 3, g, kk, None, p)
        y_pack3(state, "p", Y_AT[3], g, kk, p)

    next_substep(2, round2, t2, pf, state_g, aa, finish2)
    for n in range(3):
        sz[0, Z_AT[3] + n] = pq[16 + n]
        sz[1, Z_AT[3] + n] = pq[3 + n]
    round3 = send(3)

    arrive(round7)
    for n in range(3):
        for d, to, keep in ((0, n, klo), (1, 19 + n, khi)):
            cq[to] = rz[d, Z_AT[7] + n] * keep
    lifts()

    def tracer3(g, kk, k, state, rate):
        c = c0[3 + k] + time_step * rate
        out[0, k] = c
        growth = jnp.minimum(jnp.exp(0.3 * c), F32(3.0e38))
        ta[k] = growth
        ba[k] = jnp.sqrt(growth)

    tracer_rates(rx.at[7], ry, Y_AT[7], state_g, tracer3)

    droplets(3)
    arrive(round3)
    for n in range(3):
        for d, to, keep in ((0, n, klo), (1, 19 + n, khi)):
            pq[to] = rz[d, Z_AT[3] + n] * keep
    t3 = time_step * F32(0.25)
    round4 = first_substep(4, t3, rx.at[3], ry, Y_AT[3], state_g, state_f, aa)
    droplets(4)

    def passing(r, to):
        def finish(g, kk, k, state, p, u, v, um, vm, w):
            to[1 + k] = p
            uf[k], vf[k], umf[k], vmf[k], wf[1 + k] = u, v, um, vm, w
            narrow(r, g, kk, k, state, p)

        return finish

    next_substep(4, round4, t3, pf, state_f, aa, passing(5, pg))
    round5 = narrow_send(5, pg)
    by_depth()

    def landed(t):
        totals = [None, None, None]
        for k in range(max(t, 0), min(t + DEPTHS, L)):
            d = k - t
            grow, root = ta[k], ba[k]
            parts = (gmat[0, d, k], gmat[1, d, k] * grow, gmat[2, d, k] * grow * root)
            totals = [a if b is None else b + a for a, b in zip(parts, totals)]
        return totals

    for t in range(-8, 0):
        for m, value in enumerate(landed(t)):
            ext[m, t + 8] = value
    dropped = pltpu.make_async_remote_copy(
        src_ref=ext, dst_ref=fall, send_sem=fall_sem.at[0], recv_sem=fall_sem.at[1],
        device_id={"gz": near("gz", -1)}, device_id_type=MESH,
    )
    dropped.start()
    for t in range(0, L):
        for m, value in enumerate(landed(t)):
            mom[m, t] = value

    next_substep(5, round5, t3, pg, state_f, aa, passing(6, pf))
    round6 = narrow_send(6, pf)
    dropped.wait_recv()
    for m in range(3):
        for n in range(8):
            mom[m, 8 + n] = mom[m, 8 + n] + fall[m, n] * khi

    def last(g, kk, k, state, p, u, v, um, vm, w):
        wf[1 + k] = w
        out[1, k], out[2, k], out[3, k], out[4, k] = p, u, v, w

    next_substep(6, round6, t3, pf, state_f, aa, last)

    dropped.wait_send()
    for made in (first, second, round0, round1, round2, round7, round3, round4, round5, round6):
        for c in made:
            c.wait_send()


def solution(mesh):
    sizes = (mesh.shape["gx"], mesh.shape["gy"], mesh.shape["gz"])
    nx, ny, nz = sizes
    vm = lambda *shape: pltpu.VMEM(shape + (8, 128), F32)
    dma = pltpu.SemaphoreType.DMA
    scratch = [
        vm(5, L), pltpu.VMEM((128, 128), jnp.int32), pltpu.VMEM((8, 8, 16), jnp.int32),
        pltpu.VMEM((8 * PITCH, 128), F32), pltpu.VMEM((8 * PITCH, 128), F32), pltpu.VMEM((8 * PITCH, 128), jnp.int32),
        pltpu.VMEM((8, 8, 128), jnp.int32), pltpu.VMEM((128 * 24, 128), F32), vm(3, DEPTHS, L), vm(3, 8), vm(3, 8),
        vm(22), vm(22), vm(17), vm(22), vm(22), vm(2),
        vm(16), vm(16), vm(16), vm(16), vm(16), vm(17), vm(16), vm(16), vm(16), vm(16),
        vm(16), vm(17), vm(18), vm(18), vm(16), vm(16), vm(16), vm(16), vm(17), vm(16), vm(16), vm(16), vm(16), vm(17),
        vm(2, 2), vm(2, 12),
        vm(8, 2, 2), vm(8, 2, 2), vm(2, Y_ALL), vm(2, Y_ALL), vm(2, Z_ALL), vm(2, Z_ALL),
        pltpu.VMEM((1, 128), F32), pltpu.VMEM((nx * nz - 1, 1, 128), F32),
        pltpu.VMEM((1, 128), F32), pltpu.VMEM((ny - 1, 1, 128), F32),
        dma((8, 6)), dma((8, 6)), dma((nx * nz - 1,)), dma((nx * nz - 1,)), dma((ny - 1,)), dma((ny - 1,)),
        dma((2,)), dma((3, 8)), dma((3,)),
    ]
    vmem = pl.BlockSpec(memory_space=pltpu.VMEM)
    hbm = pl.BlockSpec(memory_space=pl.ANY)

    def per_device(fields, radius, weight, column, counts, fall_depth):
        held = pl.pallas_call(
            functools.partial(kernel, sizes),
            out_shape=(pltpu.VMEM((5, L, 8, 128), F32), pltpu.VMEM((3, L, 8, 128), F32)),
            in_specs=[hbm] * 6,
            out_specs=(vmem, vmem),
            scratch_shapes=scratch,
            compiler_params=pltpu.CompilerParams(collective_id=0, has_side_effects=True),
            name="slab_step",
        )(
            fields,
            counts.reshape(128, 128),
            jnp.transpose(fall_depth[:, :, :, 0], (0, 2, 1)),
            radius.reshape(1024, 128),
            weight.reshape(1024, 128),
            column.reshape(1024, 128),
        )
        return held

    cut = P(None, "gz", "gy", "gx")
    return jax.shard_map(
        per_device,
        mesh=mesh,
        in_specs=(cut, cut, cut, cut, P("gz", "gy", "gx"), cut),
        out_specs=(cut, cut),
        check_vma=False,
    )
```

time: 59.5 us -> 51.2 us (0.86)
  Pallas kernels: 55.4 us -> 48.7 us
  local copies, waits for them, and re-layouts: 2.44 us -> 1.4 us
    pallas_call x1, Pallas kernels: 55.4 us -> 48.7 us  [per_device(): pl.pallas_call(functools.partial(kernel, sizes), out_shape=(pltpu.VMEM((5...]
    unnamed x4 -> x2, local copies, waits for them, and re-layouts: 2.44 us -> 1.4 us
where the time goes in v1:
time: 51.2 us; the launch traced here: 50.7 us
  Pallas kernels  48.7 us (95%)
  local copies, waits for them, and re-layouts  1.4 us (3%)
  between operations  0.64 us (1%)
    pallas_call x1, Pallas kernels, per_device(): pl.pallas_call(functools.partial(kernel, sizes), out_shape=(pltpu.VMEM((5...  48.7 us
    unnamed x2, local copies, waits for them, and re-layouts  1.4 us

profile of v1, /device:TPU:1, one launch (start us, length us, event | category | flops | bytes accessed | tf_op | source)
XLA Modules:
  0.0 50.7 jit_solution(15966163974320342840)
XLA Ops:
  0.6 48.7 %slab_step.1 = (f32[5,16,8,128]{3,2,1,0:T(8,128)S(1)}, f32[3,16,8,128]{3,2,1,0:T(8,128)S(1)}) custom-call(f32[5,16,8,128]{3,2,1,0:T(8,128)} %fields_h.1, s32[128,128]{1,0:T(8,128)} %bitcast.10, s32[8,8,16]{2,1,0:T(8,128)} %bitcast.11, f32[1024,128]{1,0:T(8,128)} %bitcast.7, f32[1024,128]{1,0:T(8,128)} %bitcast.8, s32[1024,128]{1,0:T(8,128)} %bitcast.9), custom_call_target="tpu_custom_call" | custom-call | tf_op jit(solution)/shard_map/slab_step/pallas_call | solution.py:624
  49.3 0.7 %copy.10 = f32[5,16,8,128]{3,2,1,0:T(8,128)} copy(f32[5,16,8,128]{3,2,1,0:T(8,128)S(1)} %get-tuple-element.2) | data formatting | bytes 655360
  50.1 0.7 %copy.11 = f32[3,16,8,128]{3,2,1,0:T(8,128)} copy(f32[3,16,8,128]{3,2,1,0:T(8,128)S(1)} %get-tuple-element.3) | data formatting | bytes 393216

commit v2 on v1

--- a/solution.py
+++ b/solution.py
@@ -12,12 +12,13 @@
 L = 16
 DEPTHS = 9
 PITCH = 136
-Y_TILES = {0: (14, 12), 1: (18, 18), 7: (6, 6), 3: (6, 6), 2: (2, 2), 4: (2, 2), 5: (2, 2), 6: (2, 2)}
-Z_TILES = {0: (7, 6), 1: (9, 9), 7: (3, 3), 3: (3, 3), 2: (1, 1), 4: (1, 1), 5: (1, 1), 6: (1, 1)}
-Y_AT = {0: 0, 1: 14, 7: 32, 3: 38, 2: 44, 4: 46, 5: 48, 6: 50}
-Z_AT = {0: 0, 1: 7, 7: 16, 3: 19, 2: 22, 4: 23, 5: 24, 6: 25}
-Y_ALL, Z_ALL = 52, 26
-SPLITS = (0, 24, 58, 80, 100, 128)
+Y_TILES = {0: (14, 12), 1: (18, 18), 7: (6, 6), 3: (6, 6), 2: (2, 2), 5: (2, 2), 4: (10, 10)}
+Z_TILES = {0: (7, 6), 1: (9, 9), 7: (3, 3), 3: (3, 3), 2: (1, 1), 5: (1, 1), 4: (5, 5)}
+Y_AT = {0: 0, 1: 14, 7: 32, 3: 38, 2: 44, 5: 46, 4: 48}
+Z_AT = {0: 0, 1: 7, 7: 16, 3: 19, 2: 22, 5: 23, 4: 24}
+Y_ALL, Z_ALL = 58, 29
+SPLITS = (0, 56, 128)
+ROWS = 4
 
 
 def kernel(
@@ -27,11 +28,11 @@
     fields, counts, depth_in, rad, wgt, col, dep, dmat, gmat, ext, fall,
     c0, p0, w0, cq, pq, peak,
     ta, aa, ba, uinc, vinc, winc, um0, vm0, uminc, vminc,
-    tr, lift, pf, pg, uf, vf, umf, vmf, wf, ug, vg, umg, vmg, wg,
-    hx, hy,
-    sx, rx, sy, ry, sz, rz,
+    tr, lift, pf, uf, vf, umf, vmf, wf, ug, vg, umg, vmg, wg,
+    hx, hy, ep, eg, ek, en,
+    sx, rx, sy, ry, sz, rz, syz, rxy, rxz, ryz, rcorner,
     m1s, m1r, m2s, m2r,
-    send_sem, recv_sem, m1_send, m1_recv, m2_send, m2_recv, fall_sem, load_sem, field_sem,
+    send_sem, recv_sem, edge_send, edge_recv, m1_send, m1_recv, m2_send, m2_recv, fall_sem, load_sem, field_sem,
 ):
     nx, ny, nz = sizes
     ix, iy, iz = lax.axis_index("gx"), lax.axis_index("gy"), lax.axis_index("gz")
@@ -40,15 +41,26 @@
         i, n = {"gx": (ix, nx), "gy": (iy, ny), "gz": (iz, nz)}[axis]
         return lax.rem(i + (step + n), n)
 
-    group1 = [(a, b) for a in range(nx) for b in range(nz) if (a, b) != (0, 0)]
-    group2 = list(range(1, ny))
+    def device(a=0, b=0, c=0):
+        return {"gx": near("gx", a), "gy": near("gy", b), "gz": near("gz", c)}
+
+    flip = 1 - 2 * lax.rem(iy, 2)
+    group1 = [(a, f, b) for a in range(nx) for f in range(2) for b in range(nz) if (a, f, b) != (0, 0, 0)]
+    group2 = [2 * n for n in range(1, ny // 2)]
+    both = (0, 1)
+    edges = [(a, b, None) for a in both for b in both]
+    edges += [(a, None, c) for a in both for c in both]
+    edges += [(None, b, c) for b in both for c in both]
+    edges += [(a, b, c) for a in both for b in both for c in both]
+
+    def edge_device(edge):
+        return device(*(0 if d is None else 1 - 2 * d for d in edge))
+
+    partners = [device(a, f * flip, b) for a, f, b in group1] + [device(0, a) for a in group2]
+    partners += [device(0, 1), device(0, -1)] + [edge_device(e) for e in edges if e[1] is not None]
     barrier = pltpu.get_barrier_semaphore()
-    for a in group2:
-        pl.semaphore_signal(barrier, inc=1, device_id={"gy": near("gy", a)}, device_id_type=MESH)
-    for a, b in group1:
-        pl.semaphore_signal(
-            barrier, inc=1, device_id={"gx": near("gx", a), "gz": near("gz", b)}, device_id_type=MESH
-        )
+    for partner in reversed(partners):
+        pl.semaphore_signal(barrier, inc=1, device_id=partner, device_id_type=MESH)
 
     early = [
         pltpu.make_async_copy(src, dst, field_sem.at[n])
@@ -175,6 +187,19 @@
                 state[key] = moved if kk == 0 else jnp.where(row >= kk, moved, state[key])
                 if kk == 7:
                     sy[d, start + g] = state[key]
+
+    def y_pack2(state, name, start, g, kk, q):
+        t, o = divmod(2 * kk, 8)
+        for d, by in ((0, o - 6), (1, o)):
+            key = (name, d)
+            moved = roll_s(q, by)
+            state[key] = moved if o == 0 else jnp.where(row >= o, moved, state[key])
+            if o == 6:
+                sy[d, start + g * 2 + t] = state[key]
+
+    def y_halo2(ref, start, g, kk):
+        t, o = divmod(2 * kk, 8)
+        return [roll_s(ref[d, start + g * 2 + t], 6 - o if d == 0 else -o) for d in range(2)]
 
     def x_halos(mx, g, kk):
         lo, hi = mx[0, g], mx[1, g]
@@ -245,7 +270,7 @@
                 jnp.where(
                     jnp.broadcast_to(c[s : s + 1, :], (128, 128)).astype(jnp.bfloat16) == target,
                     jnp.bfloat16(1.0), jnp.bfloat16(0.0),
-                )
+                ).astype(jnp.float8_e4m3fn)
                 for s in range(8)
             ],
             axis=1,
@@ -256,14 +281,14 @@
 
     def droplets(part):
         def step(i, carry):
-            deposit_row(i * 2)
-            deposit_row(i * 2 + 1)
+            for n in range(ROWS):
+                deposit_row(i * ROWS + n)
             return carry
 
-        lax.fori_loop(SPLITS[part] // 2, SPLITS[part + 1] // 2, step, 0)
+        lax.fori_loop(SPLITS[part] // ROWS, SPLITS[part + 1] // ROWS, step, 0)
 
     def by_depth():
-        def step(k, carry):
+        def level(k):
             deep = []
             for s in range(8):
                 moved = pltpu.roll(dep[s], lax.rem(128 - k, 128), 1)
@@ -275,18 +300,22 @@
                     for s in range(1, 8):
                         total = total + jnp.where(deep[s] == d, got[s], 0.0)
                     gmat[m, d, k] = total
+
+        def step(i, carry):
+            level(2 * i)
+            level(2 * i + 1)
             return carry
 
-        lax.fori_loop(0, L, step, 0)
-
-    pl.semaphore_wait(barrier, len(group1) + len(group2))
+        lax.fori_loop(0, L // 2, step, 0)
+
+    pl.semaphore_wait(barrier, len(partners))
 
     first = []
-    for o, (a, b) in enumerate(group1):
+    for o, (a, f, b) in enumerate(group1):
         first.append(
             pltpu.make_async_remote_copy(
                 src_ref=m1s, dst_ref=m1r.at[o], send_sem=m1_send.at[o], recv_sem=m1_recv.at[o],
-                device_id={"gx": near("gx", a), "gz": near("gz", b)}, device_id_type=MESH,
+                device_id=device(a, f * flip, b), device_id_type=MESH,
             )
         )
     for c in first:
@@ -315,6 +344,23 @@
         line = [q[k + n] for n in range(7)]
         total = total + (flux(w, line[1:]) - flux(wm, line[:-1]))
         return total * F32(-1.0 / 60.0)
+
+    for c in first:
+        c.wait_recv()
+    top = m1s[...]
+    for o in range(len(group1)):
+        top = jnp.maximum(top, m1r[o])
+    m2s[...] = top
+    second = []
+    for o, a in enumerate(group2):
+        second.append(
+            pltpu.make_async_remote_copy(
+                src_ref=m2s, dst_ref=m2r.at[o], send_sem=m2_send.at[o], recv_sem=m2_recv.at[o],
+                device_id=device(0, a), device_id_type=MESH,
+            )
+        )
+    for c in second:
+        c.start()
 
     arrive(round0)
     for n in range(3):
@@ -361,23 +407,6 @@
             sz[1, Z_AT[1] + 3 * i + n] = a[n]
     round1 = send(1)
 
-    for c in first:
-        c.wait_recv()
-    top = m1s[...]
-    for o in range(len(group1)):
-        top = jnp.maximum(top, m1r[o])
-    m2s[...] = top
-    second = []
-    for o, a in enumerate(group2):
-        second.append(
-            pltpu.make_async_remote_copy(
-                src_ref=m2s, dst_ref=m2r.at[o], send_sem=m2_send.at[o], recv_sem=m2_recv.at[o],
-                device_id={"gy": near("gy", a)}, device_id_type=MESH,
-            )
-        )
-    for c in second:
-        c.start()
-
     droplets(1)
 
     for c in second:
@@ -507,7 +536,7 @@
         sz[0, Z_AT[7] + n] = tr[13 + n]
         sz[1, Z_AT[7] + n] = tr[n]
     round7 = send(7)
-    droplets(2)
+    by_depth()
 
     def finish2(g, kk, k, state, p, u, v, um, vm, w):
         pq[3 + k] = p
@@ -526,7 +555,20 @@
     for n in range(3):
         for d, to, keep in ((0, n, klo), (1, 19 + n, khi)):
             cq[to] = rz[d, Z_AT[7] + n] * keep
+    t3 = time_step * F32(0.25)
+    s10 = t3 * 10.0
+    alpha = s10 * s10
     lifts()
+
+    def forcing(g, kk, k, state):
+        value = (lift[1 + k] - lift[k]) * (-0.1 * alpha)
+        ek[0, 3 + k] = value
+        narrow(5, g, kk, k, state, value)
+
+    by_level(forcing)
+    sz[0, Z_AT[5]] = ek[0, 18]
+    sz[1, Z_AT[5]] = ek[0, 3]
+    round5 = send(5)
 
     def tracer3(g, kk, k, state, rate):
         c = c0[3 + k] + time_step * rate
@@ -536,27 +578,6 @@
         ba[k] = jnp.sqrt(growth)
 
     tracer_rates(rx.at[7], ry, Y_AT[7], state_g, tracer3)
-
-    droplets(3)
-    arrive(round3)
-    for n in range(3):
-        for d, to, keep in ((0, n, klo), (1, 19 + n, khi)):
-            pq[to] = rz[d, Z_AT[3] + n] * keep
-    t3 = time_step * F32(0.25)
-    round4 = first_substep(4, t3, rx.at[3], ry, Y_AT[3], state_g, state_f, aa)
-    droplets(4)
-
-    def passing(r, to):
-        def finish(g, kk, k, state, p, u, v, um, vm, w):
-            to[1 + k] = p
-            uf[k], vf[k], umf[k], vmf[k], wf[1 + k] = u, v, um, vm, w
-            narrow(r, g, kk, k, state, p)
-
-        return finish
-
-    next_substep(4, round4, t3, pf, state_f, aa, passing(5, pg))
-    round5 = narrow_send(5, pg)
-    by_depth()
 
     def landed(t):
         totals = [None, None, None]
@@ -570,6 +591,61 @@
     for t in range(-8, 0):
         for m, value in enumerate(landed(t)):
             ext[m, t + 8] = value
+
+    arrive(round3)
+    for n in range(3):
+        for d, to, keep in ((0, n, klo), (1, 19 + n, khi)):
+            pq[to] = rz[d, Z_AT[3] + n] * keep
+
+    wf[0] = w0[0] + t3 * (winc[0] + lift[0])
+
+    def open3(g, kk, k, state):
+        winds = (ug[k], umg[k], vg[k], vmg[k], wg[1 + k], wg[k])
+        rate = advect(pq, k, x_halo(rx.at[3], 3, g, kk), y_halo3(ry, Y_AT[3], g, kk), winds)
+        u = fields[2, k] + t3 * uinc[k]
+        um = um0[k] + t3 * uminc[k]
+        v = fields[3, k] + t3 * vinc[k]
+        vm = vm0[k] + t3 * vminc[k]
+        w = w0[1 + k] + t3 * (winc[1 + k] + lift[1 + k])
+        wm = w0[k] + t3 * (winc[k] + lift[k])
+        e = t3 * (rate - 10.0 * ((u - um) + (v - vm) + (w - wm)))
+        p = p0[3 + k] + e
+        e = e + ek[0, 3 + k]
+        ep[0, 3 + k], eg[0, 3 + k] = p, e
+        uf[k], vf[k], wf[1 + k] = u, v, w
+        x_pack(state, 4, g, kk, p, e)
+        y_pack3(state, "p", Y_AT[4], g, kk, p)
+        y_pack2(state, "e", Y_AT[4] + 6, g, kk, e)
+
+    by_level(open3)
+    for n in range(3):
+        sz[0, Z_AT[4] + n] = ep[0, 16 + n]
+        sz[1, Z_AT[4] + n] = ep[0, 3 + n]
+    for n in range(2):
+        sz[0, Z_AT[4] + 3 + n] = eg[0, 17 + n]
+        sz[1, Z_AT[4] + 3 + n] = eg[0, 3 + n]
+    for d in range(2):
+        syz[d, 0, 0] = sy[d, Y_AT[4] + 5]
+        syz[d, 0, 1] = sy[d, Y_AT[4] + 9]
+        syz[d, 1, 0] = sy[d, Y_AT[4]]
+        syz[d, 1, 1] = sy[d, Y_AT[4] + 6]
+    round4 = send(4)
+    for i, (a, b, c) in enumerate(edges):
+        if c is None:
+            src, dst = sx.at[4, a], rxy.at[a, b]
+        elif b is None:
+            src, dst = sx.at[4, a, 1 - c], rxz.at[a, c]
+        elif a is None:
+            src, dst = syz.at[b, c], ryz.at[b, c]
+        else:
+            src, dst = sx.at[4, a, 1 - c], rcorner.at[a, b, c]
+        round4.append(
+            pltpu.make_async_remote_copy(
+                src_ref=src, dst_ref=dst, send_sem=edge_send.at[i], recv_sem=edge_recv.at[i],
+                device_id=edge_device((a, b, c)), device_id_type=MESH,
+            )
+        )
+        round4[-1].start()
     dropped = pltpu.make_async_remote_copy(
         src_ref=ext, dst_ref=fall, send_sem=fall_sem.at[0], recv_sem=fall_sem.at[1],
         device_id={"gz": near("gz", -1)}, device_id_type=MESH,
@@ -579,21 +655,121 @@
         for m, value in enumerate(landed(t)):
             mom[m, t] = value
 
-    next_substep(5, round5, t3, pg, state_f, aa, passing(6, pf))
-    round6 = narrow_send(6, pf)
+    def join_l(lo, hi):
+        return jnp.where(lane < 64, hi, lo)
+
+    def join_s(lo, hi):
+        return jnp.where(row < 4, hi, lo)
+
+    def x_one(tile, d, at, kk):
+        return roll_l(tile, 125 - at - 16 * kk if d == 0 else -at - 16 * kk)
+
+    arrive(round5)
+    arrive(round4)
+
+    def assemble(g, kk, k, state):
+        at = 3 + k
+        ep[1, at] = join_s(*y_halo3(ry, Y_AT[4], g, kk))
+        eg[1, at] = join_s(*y_halo2(ry, Y_AT[4] + 6, g, kk))
+        ek[1, at] = join_s(roll_s(ry[0, Y_AT[5] + g], 7 - kk), roll_s(ry[1, Y_AT[5] + g], -kk))
+        for off, ref in ((0, ep), (3, eg)):
+            ref[2, at] = join_l(*(x_one(rx[4, d, g], d, off, kk) for d in both))
+            ref[3, at] = join_s(*(join_l(*(x_one(rxy[d, b, g], d, off, kk) for d in both)) for b in both))
+        ek[2, at] = join_l(*x_halo(rx.at[5], 3, g, kk))
+
+    by_level(assemble)
+    for n in range(3):
+        ep[0, n] = rz[0, Z_AT[4] + n]
+        ep[0, 19 + n] = rz[1, Z_AT[4] + n]
+    for n in range(2):
+        eg[0, 1 + n] = rz[0, Z_AT[4] + 3 + n]
+        eg[0, 19 + n] = rz[1, Z_AT[4] + 3 + n]
+    ek[0, 2] = rz[0, Z_AT[5]]
+    ek[0, 19] = rz[1, Z_AT[5]]
+    for c, levels in ((0, ((1, 6), (2, 7))), (1, ((19, 0), (20, 1)))):
+        for to, kk in levels:
+            t, o = divmod(3 * kk, 8)
+            ep[1, to] = join_s(roll_s(ryz[0, c, 0], 5 - o), roll_s(ryz[1, c, 0], -o))
+            ep[2, to] = join_l(*(x_one(rxz[d, c], d, 0, kk) for d in both))
+            if to in (2, 19):
+                o = (2 * kk) % 8
+                eg[1, to] = join_s(roll_s(ryz[0, c, 1], 6 - o), roll_s(ryz[1, c, 1], -o))
+                eg[2, to] = join_l(*(x_one(rxz[d, c], d, 3, kk) for d in both))
+                ep[3, to] = join_s(*(join_l(*(x_one(rcorner[d, b, c], d, 0, kk) for d in both)) for b in both))
+
+    other_x, other_y = (2, 3, 0, 1), (1, 0, 3, 2)
+
+    def neighbours(ref, part, at):
+        q, hx_, hy_ = ref[part, at], ref[other_x[part], at], ref[other_y[part], at]
+        return q, xp(q, hx_, 1), xm(q, hx_, 1), yp(q, hy_, 1), ym(q, hy_, 1)
+
+    def laplacian(ref, part, at, low=None, high=None):
+        q, a, b, c, d = neighbours(ref, part, at)
+        up, down = masked(ref[part, at + 1] - q, high), masked(q - ref[part, at - 1], low)
+        return q, (a - q, c - q, up), ((a - q) - (q - b)) + ((c - q) - (q - d)) + (up - down)
+
+    def edge_masks(at, g, kk):
+        low = jnp.where(g == 0, klo, F32(1.0)) if kk == 0 else None
+        return low, lid_at(g, kk)
+
+    def winds3(k, steps):
+        uf[k] = uf[k] - s10 * steps[0]
+        vf[k] = vf[k] - s10 * steps[1]
+        wf[1 + k] = wf[1 + k] + t3 * lift[1 + k] - s10 * steps[2]
+
+    def second3(part, at, low=None, high=None):
+        q, steps, lap = laplacian(ep, part, at, low, high)
+        e = eg[part, at] + alpha * lap
+        eg[part, at] = e
+        en[part, at] = q + e
+        return steps
+
+    def two(g, kk, k, state):
+        low, high = edge_masks(3 + k, g, kk)
+        winds3(k, second3(0, 3 + k, low, high))
+        for part in (1, 2, 3):
+            second3(part, 3 + k, low, high)
+
+    by_level(two)
+    second3(0, 1)
+    second3(0, 20)
+    for part in (0, 1, 2):
+        second3(part, 2, None, klo)
+        second3(part, 19, khi, None)
+
+    def third3(part, at, low=None, high=None):
+        q, steps, lap = laplacian(en, part, at, low, high)
+        e = eg[part, at] + ek[part, at] + alpha * lap
+        eg[part, at] = e
+        ep[part, at] = q + e
+        return steps
+
+    def three(g, kk, k, state):
+        low, high = edge_masks(3 + k, g, kk)
+        winds3(k, third3(0, 3 + k, low, high))
+        for part in (1, 2):
+            third3(part, 3 + k, low, high)
+
+    by_level(three)
+    third3(0, 2, None, klo)
+    third3(0, 19, khi, None)
+
+    def four(g, kk, k, state):
+        low, high = edge_masks(3 + k, g, kk)
+        q, steps, lap = laplacian(ep, 0, 3 + k, low, high)
+        out[1, k] = q + (eg[0, 3 + k] + ek[0, 3 + k] + alpha * lap)
+        out[2, k] = uf[k] - s10 * steps[0]
+        out[3, k] = vf[k] - s10 * steps[1]
+        out[4, k] = wf[1 + k] + t3 * lift[1 + k] - s10 * steps[2]
+
+    by_level(four)
+
     dropped.wait_recv()
     for m in range(3):
         for n in range(8):
             mom[m, 8 + n] = mom[m, 8 + n] + fall[m, n] * khi
-
-    def last(g, kk, k, state, p, u, v, um, vm, w):
-        wf[1 + k] = w
-        out[1, k], out[2, k], out[3, k], out[4, k] = p, u, v, w
-
-    next_substep(6, round6, t3, pf, state_f, aa, last)
-
     dropped.wait_send()
-    for made in (first, second, round0, round1, round2, round7, round3, round4, round5, round6):
+    for made in (first, second, round0, round1, round2, round7, round3, round4, round5):
         for c in made:
             c.wait_send()
 
@@ -609,12 +785,14 @@
         pltpu.VMEM((8, 8, 128), jnp.int32), pltpu.VMEM((128 * 24, 128), F32), vm(3, DEPTHS, L), vm(3, 8), vm(3, 8),
         vm(22), vm(22), vm(17), vm(22), vm(22), vm(2),
         vm(16), vm(16), vm(16), vm(16), vm(16), vm(17), vm(16), vm(16), vm(16), vm(16),
-        vm(16), vm(17), vm(18), vm(18), vm(16), vm(16), vm(16), vm(16), vm(17), vm(16), vm(16), vm(16), vm(16), vm(17),
-        vm(2, 2), vm(2, 12),
+        vm(16), vm(17), vm(18), vm(16), vm(16), vm(16), vm(16), vm(17), vm(16), vm(16), vm(16), vm(16), vm(17),
+        vm(2, 2), vm(2, 12), vm(4, 22), vm(4, 22), vm(4, 22), vm(4, 22),
         vm(8, 2, 2), vm(8, 2, 2), vm(2, Y_ALL), vm(2, Y_ALL), vm(2, Z_ALL), vm(2, Z_ALL),
-        pltpu.VMEM((1, 128), F32), pltpu.VMEM((nx * nz - 1, 1, 128), F32),
-        pltpu.VMEM((1, 128), F32), pltpu.VMEM((ny - 1, 1, 128), F32),
-        dma((8, 6)), dma((8, 6)), dma((nx * nz - 1,)), dma((nx * nz - 1,)), dma((ny - 1,)), dma((ny - 1,)),
+        vm(2, 2, 2), vm(2, 2, 2), vm(2, 2), vm(2, 2, 2), vm(2, 2, 2),
+        pltpu.VMEM((1, 128), F32), pltpu.VMEM((2 * nx * nz - 1, 1, 128), F32),
+        pltpu.VMEM((1, 128), F32), pltpu.VMEM((ny // 2 - 1, 1, 128), F32),
+        dma((8, 6)), dma((8, 6)), dma((20,)), dma((20,)),
+        dma((2 * nx * nz - 1,)), dma((2 * nx * nz - 1,)), dma((ny // 2 - 1,)), dma((ny // 2 - 1,)),
         dma((2,)), dma((3, 8)), dma((3,)),
     ]
     vmem = pl.BlockSpec(memory_space=pltpu.VMEM)

time: 51.2 us -> 46.6 us (0.910)
  Pallas kernels: 48.7 us -> 44.4 us
    pallas_call x1, Pallas kernels: 48.7 us -> 44.4 us  [per_device(): pl.pallas_call(functools.partial(kernel, sizes), out_shape=(pltpu.VMEM((5...]
where the time goes in v2:
time: 46.6 us; the launch traced here: 46.4 us
  Pallas kernels  44.4 us (95%)
  local copies, waits for them, and re-layouts  1.4 us (3%)
  between operations  0.64 us (1%)
    pallas_call x1, Pallas kernels, per_device(): pl.pallas_call(functools.partial(kernel, sizes), out_shape=(pltpu.VMEM((5...  44.4 us
    unnamed x2, local copies, waits for them, and re-layouts  1.4 us

profile of v2, /device:TPU:1, one launch (start us, length us, event | category | flops | bytes accessed | tf_op | source)
XLA Modules:
  0.0 46.4 jit_solution(7127918803798959921)
XLA Ops:
  0.6 44.4 %slab_step.1 = (f32[5,16,8,128]{3,2,1,0:T(8,128)S(1)}, f32[3,16,8,128]{3,2,1,0:T(8,128)S(1)}) custom-call(f32[5,16,8,128]{3,2,1,0:T(8,128)} %fields_h.1, s32[128,128]{1,0:T(8,128)} %bitcast.10, s32[8,8,16]{2,1,0:T(8,128)} %bitcast.11, f32[1024,128]{1,0:T(8,128)} %bitcast.7, f32[1024,128]{1,0:T(8,128)} %bitcast.8, s32[1024,128]{1,0:T(8,128)} %bitcast.9), custom_call_target="tpu_custom_call" | custom-call | tf_op jit(solution)/shard_map/slab_step/pallas_call | solution.py:802
  45.0 0.7 %copy.10 = f32[5,16,8,128]{3,2,1,0:T(8,128)} copy(f32[5,16,8,128]{3,2,1,0:T(8,128)S(1)} %get-tuple-element.2) | data formatting | bytes 655360
  45.7 0.7 %copy.11 = f32[3,16,8,128]{3,2,1,0:T(8,128)} copy(f32[3,16,8,128]{3,2,1,0:T(8,128)S(1)} %get-tuple-element.3) | data formatting | bytes 393216

commit v3 on v2

--- a/solution.py
+++ b/solution.py
@@ -12,9 +12,9 @@
 L = 16
 DEPTHS = 9
 PITCH = 136
-Y_TILES = {0: (14, 12), 1: (18, 18), 7: (6, 6), 3: (6, 6), 2: (2, 2), 5: (2, 2), 4: (10, 10)}
+Y_TILES = {0: (14, 12), 1: (12, 12), 6: (6, 6), 7: (6, 6), 3: (6, 6), 2: (2, 2), 5: (2, 2), 4: (10, 10)}
 Z_TILES = {0: (7, 6), 1: (9, 9), 7: (3, 3), 3: (3, 3), 2: (1, 1), 5: (1, 1), 4: (5, 5)}
-Y_AT = {0: 0, 1: 14, 7: 32, 3: 38, 2: 44, 5: 46, 4: 48}
+Y_AT = {0: 0, 1: 14, 6: 26, 7: 32, 3: 38, 2: 44, 5: 46, 4: 48}
 Z_AT = {0: 0, 1: 7, 7: 16, 3: 19, 2: 22, 5: 23, 4: 24}
 Y_ALL, Z_ALL = 58, 29
 SPLITS = (0, 56, 128)
@@ -30,9 +30,9 @@
     ta, aa, ba, uinc, vinc, winc, um0, vm0, uminc, vminc,
     tr, lift, pf, uf, vf, umf, vmf, wf, ug, vg, umg, vmg, wg,
     hx, hy, ep, eg, ek, en,
-    sx, rx, sy, ry, sz, rz, syz, rxy, rxz, ryz, rcorner,
+    sx, rx, sy, ry, sz, rz, syz, sxy, scorner, rxy, rxz, ryz, rcorner, xy,
     m1s, m1r, m2s, m2r,
-    send_sem, recv_sem, edge_send, edge_recv, m1_send, m1_recv, m2_send, m2_recv, fall_sem, load_sem, field_sem,
+    send_sem, recv_sem, small_sem, fall_sem, load_sem, field_sem,
 ):
     nx, ny, nz = sizes
     ix, iy, iz = lax.axis_index("gx"), lax.axis_index("gy"), lax.axis_index("gz")
@@ -40,27 +40,6 @@
     def near(axis, step):
         i, n = {"gx": (ix, nx), "gy": (iy, ny), "gz": (iz, nz)}[axis]
         return lax.rem(i + (step + n), n)
-
-    def device(a=0, b=0, c=0):
-        return {"gx": near("gx", a), "gy": near("gy", b), "gz": near("gz", c)}
-
-    flip = 1 - 2 * lax.rem(iy, 2)
-    group1 = [(a, f, b) for a in range(nx) for f in range(2) for b in range(nz) if (a, f, b) != (0, 0, 0)]
-    group2 = [2 * n for n in range(1, ny // 2)]
-    both = (0, 1)
-    edges = [(a, b, None) for a in both for b in both]
-    edges += [(a, None, c) for a in both for c in both]
-    edges += [(None, b, c) for b in both for c in both]
-    edges += [(a, b, c) for a in both for b in both for c in both]
-
-    def edge_device(edge):
-        return device(*(0 if d is None else 1 - 2 * d for d in edge))
-
-    partners = [device(a, f * flip, b) for a, f, b in group1] + [device(0, a) for a in group2]
-    partners += [device(0, 1), device(0, -1)] + [edge_device(e) for e in edges if e[1] is not None]
-    barrier = pltpu.get_barrier_semaphore()
-    for partner in reversed(partners):
-        pl.semaphore_signal(barrier, inc=1, device_id=partner, device_id_type=MESH)
 
     early = [
         pltpu.make_async_copy(src, dst, field_sem.at[n])
@@ -71,11 +50,32 @@
         for s in range(8):
             loads.append(
                 pltpu.make_async_copy(
-                    src.at[pl.ds(s * 128, 128)], dst.at[pl.ds(s * PITCH, 128)], load_sem.at[a, s]
+                    src.at[pl.ds(s * 128, 128)], dst.at[pl.ds(s * PITCH, 128)], load_sem.at[a]
                 )
             )
     for c in early:
         c.start()
+
+    def device(a=0, b=0, c=0):
+        return {"gx": near("gx", a), "gy": near("gy", b), "gz": near("gz", c)}
+
+    flip = 1 - 2 * lax.rem(iy, 2)
+    group1 = [(a, f, b) for a in range(nx) for f in range(2) for b in range(nz) if (a, f, b) != (0, 0, 0)]
+    group2 = [2 * n for n in range(1, ny // 2)]
+    both = (0, 1)
+    edges = [(a, b, None) for a in both for b in both]
+    edges += [(a, None, c) for a in both for c in both]
+    edges += [(None, b, c) for b in both for c in both]
+    edges += [(a, b, c) for a in both for b in both for c in both]
+
+    def edge_device(edge):
+        return device(*(0 if d is None else 1 - 2 * d for d in edge))
+
+    partners = [device(a, f * flip, b) for a, f, b in group1] + [device(0, a) for a in group2]
+    partners += [device(0, 1), device(0, -1)] + [edge_device(e) for e in edges if e[1] is not None]
+    barrier = pltpu.get_barrier_semaphore()
+    for partner in reversed(partners):
+        pl.semaphore_signal(barrier, inc=1, device_id=partner, device_id_type=MESH)
 
     lane = lax.broadcasted_iota(jnp.int32, (8, 128), 1)
     row = lax.broadcasted_iota(jnp.int32, (8, 128), 0)
@@ -118,28 +118,39 @@
     def copies(r):
         made = []
         for d, step in ((0, 1), (1, -1)):
-            y, z = pl.ds(Y_AT[r], Y_TILES[r][d]), pl.ds(Z_AT[r], Z_TILES[r][d])
-            for i, (src, dst, axis) in enumerate(
-                ((sy.at[d, y], ry.at[d, y], "gy"), (sz.at[d, z], rz.at[d, z], "gz"), (sx.at[r, d], rx.at[r, d], "gx"))
-            ):
+            y = pl.ds(Y_AT[r], Y_TILES[r][d])
+            parts = [(sy.at[d, y], ry.at[d, y], "gy")]
+            if r in Z_TILES:
+                z = pl.ds(Z_AT[r], Z_TILES[r][d])
+                parts += [(sz.at[d, z], rz.at[d, z], "gz"), (sx.at[r, d], rx.at[r, d], "gx")]
+            for i, (src, dst, axis) in enumerate(parts):
                 made.append(
                     pltpu.make_async_remote_copy(
                         src_ref=src, dst_ref=dst,
-                        send_sem=send_sem.at[r, 2 * i + d], recv_sem=recv_sem.at[r, 2 * i + d],
+                        send_sem=send_sem.at[0], recv_sem=recv_sem.at[r],
                         device_id={axis: near(axis, step)}, device_id_type=MESH,
                     )
                 )
         return made
 
     def send(r):
-        made = copies(r)
-        for c in made:
+        for c in copies(r):
             c.start()
-        return made
+        n = sum(Y_TILES[r]) + (sum(Z_TILES[r]) + 4 if r in Z_TILES else 0) + (12 if r == 4 else 0)
+        sent.append(n)
+        return r, n
+
+    sent = []
+
+    def tiles(n, send, recv):
+        span = dmat.at[pl.ds(0, 8 * n)]
+        return pltpu.make_async_remote_copy(
+            src_ref=span, dst_ref=span, send_sem=send, recv_sem=recv, device_id=device(1), device_id_type=MESH
+        )
 
     def arrive(made):
-        for c in made:
-            c.wait_recv()
+        r, n = made
+        tiles(n, send_sem.at[0], recv_sem.at[r]).wait_recv()
 
     def x_pack(state, r, g, kk, a=None, b=None, wind=None, third=None):
         base = 16 * kk
@@ -310,19 +321,27 @@
 
     pl.semaphore_wait(barrier, len(partners))
 
+    def whole(ref, i):
+        return pltpu.make_async_remote_copy(
+            src_ref=ref, dst_ref=ref, send_sem=small_sem.at[2 * i], recv_sem=small_sem.at[2 * i + 1],
+            device_id=device(1), device_id_type=MESH,
+        )
+
     first = []
     for o, (a, f, b) in enumerate(group1):
         first.append(
             pltpu.make_async_remote_copy(
-                src_ref=m1s, dst_ref=m1r.at[o], send_sem=m1_send.at[o], recv_sem=m1_recv.at[o],
+                src_ref=m1s, dst_ref=m1r.at[o], send_sem=small_sem.at[0], recv_sem=small_sem.at[1],
                 device_id=device(a, f * flip, b), device_id_type=MESH,
             )
         )
     for c in first:
         c.start()
     round0 = send(0)
-    for c in early[1:] + loads:
+    for c in early[1:]:
         c.wait()
+    for a, (src, dst) in enumerate(((rad_h, rad), (wgt_h, wgt), (col_h, col))):
+        pltpu.make_async_copy(src, dst.at[pl.ds(0, 1024)], load_sem.at[a]).wait()
     dep[...] = jnp.zeros_like(dep)
     dep[:, :, 0:16] = depth_in[...]
     droplets(0)
@@ -345,8 +364,7 @@
         total = total + (flux(w, line[1:]) - flux(wm, line[:-1]))
         return total * F32(-1.0 / 60.0)
 
-    for c in first:
-        c.wait_recv()
+    whole(m1r, 0).wait_recv()
     top = m1s[...]
     for o in range(len(group1)):
         top = jnp.maximum(top, m1r[o])
@@ -355,7 +373,7 @@
     for o, a in enumerate(group2):
         second.append(
             pltpu.make_async_remote_copy(
-                src_ref=m2s, dst_ref=m2r.at[o], send_sem=m2_send.at[o], recv_sem=m2_recv.at[o],
+                src_ref=m2s, dst_ref=m2r.at[o], send_sem=small_sem.at[2], recv_sem=small_sem.at[3],
                 device_id=device(0, a), device_id_type=MESH,
             )
         )
@@ -397,8 +415,9 @@
         uinc[k], vinc[k], winc[1 + k], lift[1 + k] = du, dv, dw, up
         um0[k], vm0[k], uminc[k], vminc[k] = um, vm, dum, dvm
         x_pack(state, 1, g, kk, t, a, None, b)
-        for i, value in enumerate((t, a, b)):
+        for i, value in enumerate((a, b)):
             y_pack3(state, i, Y_AT[1] + 6 * i, g, kk, value)
+        y_pack3(state, "t", Y_AT[6], g, kk, t)
 
     by_level(build)
     for i, a in enumerate((ta, aa, ba)):
@@ -406,11 +425,11 @@
             sz[0, Z_AT[1] + 3 * i + n] = a[13 + n]
             sz[1, Z_AT[1] + 3 * i + n] = a[n]
     round1 = send(1)
+    round6 = send(6)
 
     droplets(1)
 
-    for c in second:
-        c.wait_recv()
+    whole(m2r, 1).wait_recv()
     top = m2s[...]
     for o in range(len(group2)):
         top = jnp.maximum(top, m2r[o])
@@ -425,8 +444,7 @@
             third = jnp.where((slot >= 3) & (slot < 6), roll_l(rx[1, d, g], -5), 0.0)
             hx[d, g] = rx[0, d, g] + t1 * (rx[1, d, g] + t1 * third)
         for n in range(6):
-            hy[d, n] = ry[d, n] + t1 * ry[d, 14 + n]
-            hy[d, 6 + n] = ry[d, 6 + n] + t1 * (ry[d, 20 + n] + t1 * ry[d, 26 + n])
+            hy[d, 6 + n] = ry[d, 6 + n] + t1 * (ry[d, 14 + n] + t1 * ry[d, 20 + n])
 
     def section1(g, kk, k, state):
         cq[3 + k] = c0[3 + k] + t1 * ta[k]
@@ -531,6 +549,10 @@
         x_pack(state, 7, g, kk, c)
         y_pack3(state, "c", Y_AT[7], g, kk, c)
 
+    arrive(round6)
+    for d in range(2):
+        for n in range(6):
+            hy[d, n] = ry[d, n] + t1 * ry[d, Y_AT[6] + n]
     tracer_rates(hx, hy, 0, state_f, tracer2)
     for n in range(3):
         sz[0, Z_AT[7] + n] = tr[13 + n]
@@ -591,6 +613,11 @@
     for t in range(-8, 0):
         for m, value in enumerate(landed(t)):
             ext[m, t + 8] = value
+    dropped = pltpu.make_async_remote_copy(
+        src_ref=ext, dst_ref=fall, send_sem=fall_sem.at[0], recv_sem=fall_sem.at[1],
+        device_id={"gz": near("gz", -1)}, device_id_type=MESH,
+    )
+    dropped.start()
 
     arrive(round3)
     for n in range(3):
@@ -625,32 +652,31 @@
         sz[0, Z_AT[4] + 3 + n] = eg[0, 17 + n]
         sz[1, Z_AT[4] + 3 + n] = eg[0, 3 + n]
     for d in range(2):
-        syz[d, 0, 0] = sy[d, Y_AT[4] + 5]
-        syz[d, 0, 1] = sy[d, Y_AT[4] + 9]
-        syz[d, 1, 0] = sy[d, Y_AT[4]]
-        syz[d, 1, 1] = sy[d, Y_AT[4] + 6]
+        syz[d, 0] = jnp.where(row < 2, roll_s(sy[d, Y_AT[4] + 9], 2), sy[d, Y_AT[4] + 5])
+        syz[d, 1] = jnp.where(row < 6, sy[d, Y_AT[4]], roll_s(sy[d, Y_AT[4] + 6], 6))
+        low, high = sx[4, d, 0], sx[4, d, 1]
+        sxy[d, 0] = jnp.where(row < 4, roll_s(low, 3), roll_s(high, 7))
+        sxy[d, 1] = jnp.where(row < 4, low, roll_s(high, 4))
+        for c, tile in ((0, high), (1, low)):
+            scorner[4 * d + c] = tile[7:8, :]
+            scorner[4 * d + 2 + c] = tile[0:1, :]
     round4 = send(4)
     for i, (a, b, c) in enumerate(edges):
         if c is None:
-            src, dst = sx.at[4, a], rxy.at[a, b]
+            src, dst = sxy.at[a, b], rxy.at[a, b]
         elif b is None:
             src, dst = sx.at[4, a, 1 - c], rxz.at[a, c]
         elif a is None:
             src, dst = syz.at[b, c], ryz.at[b, c]
         else:
-            src, dst = sx.at[4, a, 1 - c], rcorner.at[a, b, c]
-        round4.append(
-            pltpu.make_async_remote_copy(
-                src_ref=src, dst_ref=dst, send_sem=edge_send.at[i], recv_sem=edge_recv.at[i],
-                device_id=edge_device((a, b, c)), device_id_type=MESH,
-            )
-        )
-        round4[-1].start()
-    dropped = pltpu.make_async_remote_copy(
-        src_ref=ext, dst_ref=fall, send_sem=fall_sem.at[0], recv_sem=fall_sem.at[1],
-        device_id={"gz": near("gz", -1)}, device_id_type=MESH,
-    )
-    dropped.start()
+            src, dst = scorner.at[4 * a + 2 * b + c], rcorner.at[4 * a + 2 * b + c]
+        corner = None not in (a, b, c)
+        pltpu.make_async_remote_copy(
+            src_ref=src, dst_ref=dst,
+            send_sem=small_sem.at[4] if corner else send_sem.at[0],
+            recv_sem=small_sem.at[5] if corner else recv_sem.at[4],
+            device_id=edge_device((a, b, c)), device_id_type=MESH,
+        ).start()
     for t in range(0, L):
         for m, value in enumerate(landed(t)):
             mom[m, t] = value
@@ -665,17 +691,34 @@
         return roll_l(tile, 125 - at - 16 * kk if d == 0 else -at - 16 * kk)
 
     arrive(round5)
+
+    def assemble_forcing(g, kk, k, state):
+        at = 3 + k
+        ek[1, at] = join_s(roll_s(ry[0, Y_AT[5] + g], 7 - kk), roll_s(ry[1, Y_AT[5] + g], -kk))
+        ek[2, at] = join_l(*x_halo(rx.at[5], 3, g, kk))
+
+    by_level(assemble_forcing)
+    ek[0, 2] = rz[0, Z_AT[5]]
+    ek[0, 19] = rz[1, Z_AT[5]]
+    dropped.wait_recv()
+    for m in range(3):
+        for n in range(8):
+            mom[m, 8 + n] = mom[m, 8 + n] + fall[m, n] * khi
+
     arrive(round4)
+    whole(rcorner, 2).wait_recv()
+
+    for d in both:
+        xy[d, 0, 0], xy[d, 0, 1] = roll_s(rxy[d, 0], 5), roll_s(rxy[d, 0], 1)
+        xy[d, 1, 0], xy[d, 1, 1] = rxy[d, 1], roll_s(rxy[d, 1], 4)
 
     def assemble(g, kk, k, state):
         at = 3 + k
         ep[1, at] = join_s(*y_halo3(ry, Y_AT[4], g, kk))
         eg[1, at] = join_s(*y_halo2(ry, Y_AT[4] + 6, g, kk))
-        ek[1, at] = join_s(roll_s(ry[0, Y_AT[5] + g], 7 - kk), roll_s(ry[1, Y_AT[5] + g], -kk))
         for off, ref in ((0, ep), (3, eg)):
             ref[2, at] = join_l(*(x_one(rx[4, d, g], d, off, kk) for d in both))
-            ref[3, at] = join_s(*(join_l(*(x_one(rxy[d, b, g], d, off, kk) for d in both)) for b in both))
-        ek[2, at] = join_l(*x_halo(rx.at[5], 3, g, kk))
+            ref[3, at] = join_s(*(join_l(*(x_one(xy[d, b, g], d, off, kk) for d in both)) for b in both))
 
     by_level(assemble)
     for n in range(3):
@@ -684,18 +727,20 @@
     for n in range(2):
         eg[0, 1 + n] = rz[0, Z_AT[4] + 3 + n]
         eg[0, 19 + n] = rz[1, Z_AT[4] + 3 + n]
-    ek[0, 2] = rz[0, Z_AT[5]]
-    ek[0, 19] = rz[1, Z_AT[5]]
     for c, levels in ((0, ((1, 6), (2, 7))), (1, ((19, 0), (20, 1)))):
         for to, kk in levels:
             t, o = divmod(3 * kk, 8)
-            ep[1, to] = join_s(roll_s(ryz[0, c, 0], 5 - o), roll_s(ryz[1, c, 0], -o))
+            ep[1, to] = join_s(roll_s(ryz[0, c], 5 - o), roll_s(ryz[1, c], -o))
             ep[2, to] = join_l(*(x_one(rxz[d, c], d, 0, kk) for d in both))
             if to in (2, 19):
-                o = (2 * kk) % 8
-                eg[1, to] = join_s(roll_s(ryz[0, c, 1], 6 - o), roll_s(ryz[1, c, 1], -o))
+                o = 0 if c == 0 else 6
+                eg[1, to] = join_s(roll_s(ryz[0, c], 6 - o), roll_s(ryz[1, c], -o))
                 eg[2, to] = join_l(*(x_one(rxz[d, c], d, 3, kk) for d in both))
-                ep[3, to] = join_s(*(join_l(*(x_one(rcorner[d, b, c], d, 0, kk) for d in both)) for b in both))
+                ends = [
+                    join_l(*(x_one(jnp.broadcast_to(rcorner[4 * d + 2 * b + c], (8, 128)), d, 0, kk) for d in both))
+                    for b in both
+                ]
+                ep[3, to] = join_s(*ends)
 
     other_x, other_y = (2, 3, 0, 1), (1, 0, 3, 2)
 
@@ -764,14 +809,10 @@
 
     by_level(four)
 
-    dropped.wait_recv()
-    for m in range(3):
-        for n in range(8):
-            mom[m, 8 + n] = mom[m, 8 + n] + fall[m, n] * khi
     dropped.wait_send()
-    for made in (first, second, round0, round1, round2, round7, round3, round4, round5):
-        for c in made:
-            c.wait_send()
+    for i, ref in enumerate((m1r, m2r, rcorner)):
+        whole(ref, i).wait_send()
+    tiles(sum(sent), send_sem.at[0], recv_sem.at[0]).wait_send()
 
 
 def solution(mesh):
@@ -788,12 +829,11 @@
         vm(16), vm(17), vm(18), vm(16), vm(16), vm(16), vm(16), vm(17), vm(16), vm(16), vm(16), vm(16), vm(17),
         vm(2, 2), vm(2, 12), vm(4, 22), vm(4, 22), vm(4, 22), vm(4, 22),
         vm(8, 2, 2), vm(8, 2, 2), vm(2, Y_ALL), vm(2, Y_ALL), vm(2, Z_ALL), vm(2, Z_ALL),
-        vm(2, 2, 2), vm(2, 2, 2), vm(2, 2), vm(2, 2, 2), vm(2, 2, 2),
+        vm(2, 2), vm(2, 2), pltpu.VMEM((8, 1, 128), F32),
+        vm(2, 2), vm(2, 2), vm(2, 2), pltpu.VMEM((8, 1, 128), F32), vm(2, 2, 2),
         pltpu.VMEM((1, 128), F32), pltpu.VMEM((2 * nx * nz - 1, 1, 128), F32),
         pltpu.VMEM((1, 128), F32), pltpu.VMEM((ny // 2 - 1, 1, 128), F32),
-        dma((8, 6)), dma((8, 6)), dma((20,)), dma((20,)),
-        dma((2 * nx * nz - 1,)), dma((2 * nx * nz - 1,)), dma((ny // 2 - 1,)), dma((ny // 2 - 1,)),
-        dma((2,)), dma((3, 8)), dma((3,)),
+        dma((1,)), dma((8,)), dma((6,)), dma((2,)), dma((3,)), dma((3,)),
     ]
     vmem = pl.BlockSpec(memory_space=pltpu.VMEM)
     hbm = pl.BlockSpec(memory_space=pl.ANY)

time: 46.6 us -> 43.8 us (0.940)
  Pallas kernels: 44.4 us -> 41.6 us
    pallas_call x1, Pallas kernels: 44.4 us -> 41.6 us  [per_device(): pl.pallas_call(functools.partial(kernel, sizes), out_shape=(pltpu.VMEM((5...]
where the time goes in v3:
time: 43.8 us; the launch traced here: 43.7 us
  Pallas kernels  41.6 us (95%)
  local copies, waits for them, and re-layouts  1.4 us (3%)
  between operations  0.64 us (1%)
    pallas_call x1, Pallas kernels, per_device(): pl.pallas_call(functools.partial(kernel, sizes), out_shape=(pltpu.VMEM((5...  41.6 us
    unnamed x2, local copies, waits for them, and re-layouts  1.4 us

profile of v3, /device:TPU:1, one launch (start us, length us, event | category | flops | bytes accessed | tf_op | source)
XLA Modules:
  0.0 43.7 jit_solution(15607739267129614222)
XLA Ops:
  0.6 41.6 %slab_step.1 = (f32[5,16,8,128]{3,2,1,0:T(8,128)S(1)}, f32[3,16,8,128]{3,2,1,0:T(8,128)S(1)}) custom-call(f32[5,16,8,128]{3,2,1,0:T(8,128)} %fields_h.1, s32[128,128]{1,0:T(8,128)} %bitcast.10, s32[8,8,16]{2,1,0:T(8,128)} %bitcast.11, f32[1024,128]{1,0:T(8,128)} %bitcast.7, f32[1024,128]{1,0:T(8,128)} %bitcast.8, s32[1024,128]{1,0:T(8,128)} %bitcast.9), custom_call_target="tpu_custom_call" | custom-call | tf_op jit(solution)/shard_map/slab_step/pallas_call | solution.py:842
  42.3 0.7 %copy.10 = f32[5,16,8,128]{3,2,1,0:T(8,128)} copy(f32[5,16,8,128]{3,2,1,0:T(8,128)S(1)} %get-tuple-element.2) | data formatting | bytes 655360
  43.0 0.7 %copy.11 = f32[3,16,8,128]{3,2,1,0:T(8,128)} copy(f32[3,16,8,128]{3,2,1,0:T(8,128)S(1)} %get-tuple-element.3) | data formatting | bytes 393216

commit v4 on v3

--- a/solution.py
+++ b/solution.py
@@ -17,7 +17,7 @@
 Y_AT = {0: 0, 1: 14, 6: 26, 7: 32, 3: 38, 2: 44, 5: 46, 4: 48}
 Z_AT = {0: 0, 1: 7, 7: 16, 3: 19, 2: 22, 5: 23, 4: 24}
 Y_ALL, Z_ALL = 58, 29
-SPLITS = (0, 56, 128)
+SPLITS = (0, 72, 128)
 ROWS = 4
 
 
@@ -53,7 +53,9 @@
                     src.at[pl.ds(s * 128, 128)], dst.at[pl.ds(s * PITCH, 128)], load_sem.at[a]
                 )
             )
-    for c in early:
+    for n in range(5):
+        pltpu.make_async_copy(fields_h.at[n], fields.at[n], field_sem.at[0]).start()
+    for c in early[1:]:
         c.start()
 
     def device(a=0, b=0, c=0):
@@ -425,9 +427,10 @@
             sz[0, Z_AT[1] + 3 * i + n] = a[13 + n]
             sz[1, Z_AT[1] + 3 * i + n] = a[n]
     round1 = send(1)
+
+    droplets(1)
+
     round6 = send(6)
-
-    droplets(1)
 
     whole(m2r, 1).wait_recv()
     top = m2s[...]
@@ -549,6 +552,7 @@
         x_pack(state, 7, g, kk, c)
         y_pack3(state, "c", Y_AT[7], g, kk, c)
 
+    by_depth()
     arrive(round6)
     for d in range(2):
         for n in range(6):
@@ -558,7 +562,6 @@
         sz[0, Z_AT[7] + n] = tr[13 + n]
         sz[1, Z_AT[7] + n] = tr[n]
     round7 = send(7)
-    by_depth()
 
     def finish2(g, kk, k, state, p, u, v, um, vm, w):
         pq[3 + k] = p

time: 43.8 us -> 43.4 us (level)
  no operation moved by 1% of the time
where the time goes in v4:
time: 43.4 us; the launch traced here: 43.2 us
  Pallas kernels  41.2 us (95%)
  local copies, waits for them, and re-layouts  1.4 us (3%)
  between operations  0.64 us (1%)
    pallas_call x1, Pallas kernels, per_device(): pl.pallas_call(functools.partial(kernel, sizes), out_shape=(pltpu.VMEM((5...  41.2 us
    unnamed x2, local copies, waits for them, and re-layouts  1.4 us

profile of v4, /device:TPU:1, one launch (start us, length us, event | category | flops | bytes accessed | tf_op | source)
XLA Modules:
  0.0 43.2 jit_solution(9823991936532995586)
XLA Ops:
  0.6 41.2 %slab_step.1 = (f32[5,16,8,128]{3,2,1,0:T(8,128)S(1)}, f32[3,16,8,128]{3,2,1,0:T(8,128)S(1)}) custom-call(f32[5,16,8,128]{3,2,1,0:T(8,128)} %fields_h.1, s32[128,128]{1,0:T(8,128)} %bitcast.10, s32[8,8,16]{2,1,0:T(8,128)} %bitcast.11, f32[1024,128]{1,0:T(8,128)} %bitcast.7, f32[1024,128]{1,0:T(8,128)} %bitcast.8, s32[1024,128]{1,0:T(8,128)} %bitcast.9), custom_call_target="tpu_custom_call" | custom-call | tf_op jit(solution)/shard_map/slab_step/pallas_call | solution.py:845
  41.8 0.7 %copy.10 = f32[5,16,8,128]{3,2,1,0:T(8,128)} copy(f32[5,16,8,128]{3,2,1,0:T(8,128)S(1)} %get-tuple-element.2) | data formatting | bytes 655360
  42.6 0.7 %copy.11 = f32[3,16,8,128]{3,2,1,0:T(8,128)} copy(f32[3,16,8,128]{3,2,1,0:T(8,128)S(1)} %get-tuple-element.3) | data formatting | bytes 393216

commit v5 on v4

--- a/solution.py
+++ b/solution.py
@@ -663,7 +663,6 @@
         for c, tile in ((0, high), (1, low)):
             scorner[4 * d + c] = tile[7:8, :]
             scorner[4 * d + 2 + c] = tile[0:1, :]
-    round4 = send(4)
     for i, (a, b, c) in enumerate(edges):
         if c is None:
             src, dst = sxy.at[a, b], rxy.at[a, b]
@@ -680,6 +679,7 @@
             recv_sem=small_sem.at[5] if corner else recv_sem.at[4],
             device_id=edge_device((a, b, c)), device_id_type=MESH,
         ).start()
+    round4 = send(4)
     for t in range(0, L):
         for m, value in enumerate(landed(t)):
             mom[m, t] = value

time: 43.4 us -> 42.9 us (0.988)
    pallas_call x1, Pallas kernels: 41.2 us -> 40.8 us  [per_device(): pl.pallas_call(functools.partial(kernel, sizes), out_shape=(pltpu.VMEM((5...]
where the time goes in v5:
time: 42.9 us; the launch traced here: 42.8 us
  Pallas kernels  40.8 us (95%)
  local copies, waits for them, and re-layouts  1.4 us (3%)
  between operations  0.64 us (1%)
    pallas_call x1, Pallas kernels, per_device(): pl.pallas_call(functools.partial(kernel, sizes), out_shape=(pltpu.VMEM((5...  40.8 us
    unnamed x2, local copies, waits for them, and re-layouts  1.4 us

profile of v5, /device:TPU:1, one launch (start us, length us, event | category | flops | bytes accessed | tf_op | source)
XLA Modules:
  0.0 42.8 jit_solution(12445182618678685213)
XLA Ops:
  0.6 40.8 %slab_step.1 = (f32[5,16,8,128]{3,2,1,0:T(8,128)S(1)}, f32[3,16,8,128]{3,2,1,0:T(8,128)S(1)}) custom-call(f32[5,16,8,128]{3,2,1,0:T(8,128)} %fields_h.1, s32[128,128]{1,0:T(8,128)} %bitcast.10, s32[8,8,16]{2,1,0:T(8,128)} %bitcast.11, f32[1024,128]{1,0:T(8,128)} %bitcast.7, f32[1024,128]{1,0:T(8,128)} %bitcast.8, s32[1024,128]{1,0:T(8,128)} %bitcast.9), custom_call_target="tpu_custom_call" | custom-call | tf_op jit(solution)/shard_map/slab_step/pallas_call | solution.py:845
  41.4 0.7 %copy.10 = f32[5,16,8,128]{3,2,1,0:T(8,128)} copy(f32[5,16,8,128]{3,2,1,0:T(8,128)S(1)} %get-tuple-element.2) | data formatting | bytes 655360
  42.1 0.7 %copy.11 = f32[3,16,8,128]{3,2,1,0:T(8,128)} copy(f32[3,16,8,128]{3,2,1,0:T(8,128)S(1)} %get-tuple-element.3) | data formatting | bytes 393216
